TPU v7x, 128 devices: a whole 4x4x4 slice. The times are simulated.
128 devices in a mesh: gx: 16 (over x, y), gy: 8 (over z, core).
Axes of the slice: x: 4, y: 4, z: 4, core: 2. Of those that a mesh axis runs over, the one named last changes fastest.
Arguments:
- thermal_state: bfloat16 [98304, 4096], P(('gx', 'gy')), may hold values from 0.59765625 to 1.3984375
- opacity_field: bfloat16 [98304, 4096], P(('gx', 'gy')), may hold values from 0.15 to 4.5
- glowing_depth: int32 [98304], P(('gx', 'gy')), may hold values from 1 to 16
- position_to_tile: int32 [98304], P(('gx', 'gy')), may hold values from 0 to 98303, as said below
- tile_to_position: int32 [98304], P(('gx', 'gy')), may hold values from 0 to 98303, as said below
Outputs:
- heating: float32 [98304, 4096], P(('gx', 'gy'))
Inputs may be any that keep to these rules, and one draw needn't show every extreme that they name: `position_to_tile`: A permutation. Box q belongs to column q // 768. The 768 slots s with the same s // 768 hold boxes of exactly half of the 128 columns, exactly 12 boxes of each of those. tile_to_position[position_to_tile[s]] = s for every slot s.
All inputs are finite; a program needn't handle non-finite values.
Results may differ from a plain program's by a relative error of at most 0.0003.
Values sent between devices are 32-bit elements; how exact they have to be, the bound alone decides.
A program may use at most 128 MiB of HBM per device.

v0:
```python
import jax
import jax.numpy as jnp
import numpy as np
from jax import lax
from jax.sharding import Mesh
from jax.sharding import PartitionSpec as P

CB = 4
RF = 4
CX = 16
CY = 24
CZ = 128
EDGE_RESOLUTION = 16
GX = ("gx_0", "gx_1")
GY = ("gy_0", "gy_1")
GX_GY = ("gx_0", "gx_1", "gy_0", "gy_1")


EXACT_DOT = lax.Precision.HIGHEST


def in_blocks(shard, dim, size):
    shape = shard.shape
    blocks = shard.reshape(*shape[:dim], size, shape[dim] // size, *shape[dim + 1 :])
    return jnp.moveaxis(blocks, dim, 0)


def in_order(blocks, dim):
    shape = list(blocks.shape[1:])
    shape[dim] *= blocks.shape[0]
    return jnp.moveaxis(blocks, 0, dim).reshape(shape)


def one_exchange(shard, axis, axes, splits, concats):
    sizes = [lax.axis_size(a) for a in axes]
    blocks = in_blocks(shard, splits[0], sizes[0])
    blocks = jnp.moveaxis(in_blocks(blocks, splits[1] + 1, sizes[1]), 0, 1)
    inside = blocks.shape[2:]
    blocks = blocks.reshape(-1, *inside)
    blocks = lax.all_to_all(blocks, axis, split_axis=0, concat_axis=0, tiled=True)
    blocks = in_order(blocks.reshape(*sizes, *inside), concats[0] + 1)
    return in_order(blocks, concats[1])


def with_halo(block, sides, width):
    for axis, dim in sides:
        count = lax.axis_size(axis)
        forward = [(i, i + 1) for i in range(count - 1)]
        backward = [(target, source) for source, target in forward]
        low = lax.ppermute(
            lax.slice_in_dim(block, block.shape[dim] - width, None, axis=dim), axis, forward
        )
        high = lax.ppermute(lax.slice_in_dim(block, 0, width, axis=dim), axis, backward)
        block = jnp.concatenate([low, block, high], axis=dim)
    return block


def over_axes(shard, axes):
    for axis in axes:
        shard = lax.pmin(shard, axis)
    return shard


def restrict_table():
    fine_index = np.arange(EDGE_RESOLUTION**3)
    coarse_x = fine_index // (EDGE_RESOLUTION * EDGE_RESOLUTION) // RF
    coarse_y = fine_index // EDGE_RESOLUTION % EDGE_RESOLUTION // RF
    coarse_z = fine_index % EDGE_RESOLUTION // RF
    coarse_index = (coarse_x * CB + coarse_y) * CB + coarse_z
    averaging = (coarse_index[:, None] == np.arange(CB**3)[None, :]) / float(RF**3)
    return jnp.asarray(averaging, jnp.float32)


def spread_table():
    border = CB + 2
    line_weights = np.zeros((EDGE_RESOLUTION, border))
    for offset in range(EDGE_RESOLUTION):
        position = (offset + 0.5) / RF + 0.5
        lower_cell = int(np.floor(position))
        upper_share = position - lower_cell
        line_weights[offset, lower_cell] += 1.0 - upper_share
        line_weights[offset, lower_cell + 1] += upper_share
    tensor_weights = np.kron(np.kron(line_weights, line_weights), line_weights)
    return jnp.asarray(tensor_weights.T, jnp.float32)


def picker(blocks, length):
    border = CB + 2
    wanted = (
        jnp.arange(blocks, dtype=jnp.int32)[:, None] * CB
        + jnp.arange(border, dtype=jnp.int32)[None, :]
    )
    cells = jnp.arange(length, dtype=jnp.int32)
    return (wanted[:, :, None] == cells[None, None, :]).astype(jnp.float32)


def cut_windows(coarse_grid, span_x, span_y, span_z):
    border = CB + 2
    blocks_x, blocks_y, blocks_z = (span_x // CB, span_y // CB, span_z // CB)
    pick_z = picker(blocks_z, span_z + 2).reshape(blocks_z * border, span_z + 2)
    along_z = lax.dot_general(coarse_grid, pick_z, (((2,), (1,)), ((), ())), precision=EXACT_DOT)
    pick_y = picker(blocks_y, span_y + 2)
    along_y = jnp.einsum("bjy,xyn->xbjn", pick_y, along_z, precision=EXACT_DOT)
    pick_x = picker(blocks_x, span_x + 2)
    along_x = jnp.einsum("aix,xbjn->abijn", pick_x, along_y, precision=EXACT_DOT)
    along_x = along_x.reshape(blocks_x, blocks_y, border, border, blocks_z, border)
    return along_x.transpose(0, 1, 4, 2, 3, 5).reshape(-1, border**3)


def face_weight(first, second):
    return 2.0 / (3.0 * (first + second))


def bucket_rank(owner_dev, buckets):
    onehot = (owner_dev[:, None] == jnp.arange(buckets, dtype=jnp.int32)[None, :]).astype(jnp.int32)
    running = jnp.cumsum(onehot, axis=0)
    return jnp.sum(running * onehot, axis=1) - 1


def on_device(thermal_state, opacity_field, glowing_depth, position_to_tile, tile_to_position):
    across_x = lax.axis_size(GX)
    across_y = lax.axis_size(GY)
    devices = across_x * across_y
    index_x = lax.axis_index(GX)
    index_y = lax.axis_index(GY)
    stack_tiles = thermal_state.shape[0]
    slots = 2 * stack_tiles // devices
    border = CB + 2
    layer_index = jnp.arange(EDGE_RESOLUTION**3, dtype=jnp.int32) % EDGE_RESOLUTION
    emitting = (layer_index[None, :] < glowing_depth[:, None]).astype(jnp.float32)
    absorb_f = opacity_field.astype(jnp.float32)
    thermal_forcing = thermal_state.astype(jnp.float32)
    square = thermal_forcing * thermal_forcing
    fourth = square * square * emitting
    emission = absorb_f * fourth
    averaging = restrict_table()
    restricted_glow = jnp.concatenate(
        [
            jnp.dot(emission, averaging, precision=EXACT_DOT),
            jnp.dot(absorb_f, averaging, precision=EXACT_DOT),
        ],
        axis=1,
    )
    owner_dev = position_to_tile // stack_tiles
    target = owner_dev * slots + bucket_rank(owner_dev, devices)
    outgoing = (
        jnp.zeros((devices * slots, restricted_glow.shape[1]), jnp.float32)
        .at[target]
        .set(restricted_glow)
    )
    labels = (
        jnp.full((devices * slots,), -1, jnp.int32).at[target].set(position_to_tile % stack_tiles)
    )
    arrived, arrived_labels = (
        one_exchange(outgoing.reshape(across_x, -1), GX_GY, (GX, GY), (0, 1), (0, 1)),
        one_exchange(labels.reshape(across_x, -1), GX_GY, (GX, GY), (0, 1), (0, 1)),
    )
    arrived = arrived.reshape(devices * slots, -1)
    arrived_labels = arrived_labels.reshape(-1)
    placed = jnp.where(arrived_labels >= 0, arrived_labels, stack_tiles)
    box_values = (
        jnp.zeros((stack_tiles, arrived.shape[1]), jnp.float32).at[placed].set(arrived, mode="drop")
    )
    boxes_x, boxes_y, boxes_z = (CX // CB, CY // CB, CZ // CB)
    coarse_grid = box_values.reshape(boxes_x, boxes_y, boxes_z, 2, CB, CB, CB)
    coarse_grid = coarse_grid.transpose(3, 0, 4, 1, 5, 2, 6).reshape(2, CX, CY, CZ)
    source = 4.0 * coarse_grid[0]
    coarse_k = coarse_grid[1]
    margin = 4
    padded_k = with_halo(coarse_k, ((GX, 0), (GY, 1)), margin)
    coord_x = index_x * CX + jnp.arange(-margin, CX + margin, dtype=jnp.int32)
    coord_y = index_y * CY + jnp.arange(-margin, CY + margin, dtype=jnp.int32)
    inside_x = (coord_x >= 0) & (coord_x < CX * across_x)
    inside_y = (coord_y >= 0) & (coord_y < CY * across_y)
    inside = inside_x[:, None, None] & inside_y[None, :, None]
    padded_fix = jnp.where(inside, padded_k, 1.0)
    center = padded_fix[1:-1, 1:-1]
    inner_mask = inside[1:-1, 1:-1]

    def neighbour(values, flags):
        return jnp.where(flags, values, center)

    stretched_k = jnp.pad(center, ((0, 0), (0, 0), (1, 1)), mode="edge")
    minus_x = face_weight(center, neighbour(padded_fix[:-2, 1:-1], inside[:-2, 1:-1]))
    plus_x = face_weight(center, neighbour(padded_fix[2:, 1:-1], inside[2:, 1:-1]))
    minus_y = face_weight(center, neighbour(padded_fix[1:-1, :-2], inside[1:-1, :-2]))
    plus_y = face_weight(center, neighbour(padded_fix[1:-1, 2:], inside[1:-1, 2:]))
    minus_z = face_weight(center, stretched_k[:, :, :-2])
    plus_z = face_weight(center, stretched_k[:, :, 2:])
    diagonal = center + minus_x + plus_x + minus_y + plus_y + minus_z + plus_z
    inverse = jnp.where(inner_mask, 1.0 / diagonal, 0.0)
    own_at = margin - 1
    own_ratio = (
        center[own_at : own_at + CX, own_at : own_at + CY]
        / diagonal[own_at : own_at + CX, own_at : own_at + CY]
    )
    lowest = over_axes(jnp.min(own_ratio), GX_GY)
    cheb_delta = 1.0 - lowest
    cheb_sigma = 1.0 / cheb_delta
    cheb_rho = cheb_delta
    weights = (diagonal, minus_x, plus_x, minus_y, plus_y, minus_z, plus_z)
    solution = jnp.zeros((CX, CY, CZ), jnp.float32)
    direction = inverse[own_at : own_at + CX, own_at : own_at + CY] * source
    stacked = with_halo(jnp.stack([direction, source]), ((GX, 1), (GY, 2)), 4)
    search = stacked[0]
    remain = stacked[1]
    for inner_step in range(margin):
        margin_left = margin - 1 - inner_step
        width_x = CX + 2 * margin_left
        width_y = CY + 2 * margin_left
        sliced = [
            weight[inner_step : inner_step + width_x, inner_step : inner_step + width_y]
            for weight in weights
        ]
        middle = search[1:-1, 1:-1]
        stretched = jnp.pad(middle, ((0, 0), (0, 0), (1, 1)))
        applied = sliced[0] * middle - (
            sliced[1] * search[:-2, 1:-1]
            + sliced[2] * search[2:, 1:-1]
            + sliced[3] * search[1:-1, :-2]
            + sliced[4] * search[1:-1, 2:]
            + sliced[5] * stretched[:, :, :-2]
            + sliced[6] * stretched[:, :, 2:]
        )
        middle = search[1:-1, 1:-1]
        solution = solution + middle[margin_left : margin_left + CX, margin_left : margin_left + CY]
        remain = remain[1:-1, 1:-1] - applied
        rho_next = 1.0 / (2.0 * cheb_sigma - cheb_rho)
        scaled = (
            inverse[inner_step : inner_step + width_x, inner_step : inner_step + width_y] * remain
        )
        search = rho_next * cheb_rho * middle + 2.0 * rho_next / cheb_delta * scaled
        cheb_rho = rho_next
    incident = solution + search
    rimmed = with_halo(incident, ((GX, 0), (GY, 1)), 1)
    rimmed = rimmed.at[0].set(jnp.where(index_x == 0, rimmed[1], rimmed[0]))
    rimmed = rimmed.at[-1].set(jnp.where(index_x == across_x - 1, rimmed[-2], rimmed[-1]))
    rimmed = rimmed.at[:, 0].set(jnp.where(index_y == 0, rimmed[:, 1], rimmed[:, 0]))
    rimmed = rimmed.at[:, -1].set(jnp.where(index_y == across_y - 1, rimmed[:, -2], rimmed[:, -1]))
    rimmed = jnp.pad(rimmed, ((0, 0), (0, 0), (1, 1)), mode="edge")
    windows = cut_windows(rimmed, CX, CY, CZ)
    home_dev = tile_to_position // stack_tiles
    goal_row = home_dev * slots + bucket_rank(home_dev, devices)
    leaving = jnp.zeros((devices * slots, border**3), jnp.float32).at[goal_row].set(windows)
    slot_marks = (
        jnp.full((devices * slots,), -1, jnp.int32).at[goal_row].set(tile_to_position % stack_tiles)
    )
    returned, returned_marks = (
        one_exchange(leaving.reshape(across_x, -1), GX_GY, (GX, GY), (0, 1), (0, 1)),
        one_exchange(slot_marks.reshape(across_x, -1), GX_GY, (GX, GY), (0, 1), (0, 1)),
    )
    returned = returned.reshape(devices * slots, border**3)
    returned_marks = returned_marks.reshape(-1)
    slot_rows = jnp.where(returned_marks >= 0, returned_marks, stack_tiles)
    by_slot = (
        jnp.zeros((stack_tiles, border**3), jnp.float32).at[slot_rows].set(returned, mode="drop")
    )
    fine_field = jnp.dot(by_slot, spread_table(), precision=EXACT_DOT)
    return absorb_f * (fine_field - 4.0 * fourth)


def solution(mesh):
    split = Mesh(mesh.devices.reshape(4, 4, 4, 2), ("gx_0", "gx_1", "gy_0", "gy_1"))
    return jax.shard_map(
        on_device,
        mesh=split,
        in_specs=(P(GX_GY, None), P(GX_GY, None), P(GX_GY), P(GX_GY), P(GX_GY)),
        out_specs=P(GX_GY, None),
        check_vma=False,
    )
```

profile of v0, /device:TPU:1, one launch (start us, length us, event | category | flops | bytes accessed | tf_op | source)
XLA Modules:
  0.0 322.6 jit_solution(3721402644380448066)
XLA Ops:
  2.4 3.4 %scatter_custom_fusion.1 = s32[1536]{0:T(1024)S(1)} fusion(s32[768]{0:T(1024)S(1)} %get-tuple-element.88, s32[768]{0:T(1024)S(1)} %get-tuple-element.87, s32[]{:T(128)} %constant.202.clone.1), kind=kCustom, calls=%fused_computation.214 | custom fusion | bytes 6148 | tf_op jit(solution)/shard_map/scatter | solution.py:152
  6.5 11.7 %all-to-all-start.1 = ((s32[128,1,12]{2,1,0:T(1,128)}), s32[128,1,12]{2,1,0:T(1,128)S(1)}, u32[]{:S(2)}, u32[]{:S(2)}) async-start(s32[128,1,12]{2,1,0:T(1,128)} %bitcast.14), calls=%async_computation.1 | async-start | bytes 131072 | tf_op jit(solution)/shard_map/all_to_all | solution.py:40
  19.8 9.4 %convolution_bitcast_fusion.3 = f32[768,64]{0,1:T(8,128)S(1)} fusion(f32[4096,64]{1,0:T(8,128)} %constant.227.clone, bf16[768,4096]{1,0:T(8,128)(2,1)} %param.16), kind=kOutput, calls=%fused_computation.17 | convolution fusion | flops 2415919104 | bytes 7536640 | tf_op jit(solution)/shard_map/dot_general | solution.py:140
  29.3 16.6 %fusion = f32[768,64]{0,1:T(8,128)S(1)} fusion(f32[4096,64]{1,0:T(8,128)S(1)} %copy-done, bf16[768,4096]{1,0:T(8,128)(2,1)S(1)} %bitcast.122, bf16[768,4096]{1,0:T(8,128)(2,1)} %param.15, s32[4096]{0:T(1024)S(1)} %add_select_fusion, s32[768]{0:T(1024)S(1)} %copy-done.8), kind=kOutput, calls=%fused_computation.8 | convolution fusion | flops 2437939200 | bytes 13847552 | tf_op jit(solution)/shard_map/dot_general | solution.py:139
  46.1 3.4 %scatter_custom_fusion = s32[1536]{0:T(1024)S(1)} fusion(s32[768]{0:T(1024)S(1)} %get-tuple-element.92, s32[768]{0:T(1024)S(1)} %get-tuple-element.91, s32[]{:T(128)} %constant.202.clone.1), kind=kCustom, calls=%fused_computation.216 | custom fusion | bytes 6148 | tf_op jit(solution)/shard_map/scatter | solution.py:246
  50.2 5.0 %scatter_custom_fusion.2 = f32[1536,128]{1,0:T(8,128)} fusion(s32[768]{0:T(1024)S(1)} %get-tuple-element.88, f32[768,128]{1,0:T(8,128)S(1)} %copy.41, f32[]{:T(128)} %constant.201.clone.1), kind=kCustom, calls=%fused_computation.55 | custom fusion | bytes 786436 | tf_op jit(solution)/shard_map/scatter | solution.py:149
  55.3 9.8 %all-to-all-start.2 = ((f32[128,1,1536]{2,1,0:T(1,128)}), f32[128,1,1536]{2,1,0:T(1,128)S(1)}, u32[]{:S(2)}, u32[]{:S(2)}) async-start(f32[128,1,1536]{2,1,0:T(1,128)} %bitcast.20), calls=%async_computation.2 | async-start | bytes 1572864 | tf_op jit(solution)/shard_map/all_to_all | solution.py:40
  66.0 15.4 %all-to-all-done.2 = f32[128,1,1536]{2,1,0:T(1,128)S(1)} async-done(((f32[128,1,1536]{2,1,0:T(1,128)}), f32[128,1,1536]{2,1,0:T(1,128)S(1)}, u32[]{:S(2)}, u32[]{:S(2)}) %all-to-all-start.2) | async-done | bytes 786464 | tf_op jit(solution)/shard_map/all_to_all | solution.py:40
  81.4 5.6 %all-to-all-start = ((s32[128,1,12]{2,1,0:T(1,128)}), s32[128,1,12]{2,1,0:T(1,128)}, u32[]{:S(2)}, u32[]{:S(2)}) async-start(s32[128,1,12]{2,1,0:T(1,128)} %bitcast.4), calls=%async_computation | async-start | bytes 131072 | tf_op jit(solution)/shard_map/all_to_all | solution.py:40
  87.2 4.6 %scatter_custom_fusion.3 = f32[768,128]{1,0:T(8,128)S(1)} fusion(s32[1536]{0:T(1024)S(1)} %fusion.101, f32[1536,128]{1,0:T(8,128)S(1)} %reshape.452, f32[]{:T(128)} %constant.201.clone.1), kind=kCustom, calls=%fused_computation.154 | custom fusion | bytes 393220 | tf_op jit(solution)/shard_map/scatter | solution.py:162
  92.8 1.8 copy.45
  94.6 2.5 slice.426
  97.1 3.3 %collective-permute-start = (f32[4,24,128]{2,1,0:T(8,128)S(1)}, f32[4,24,128]{2,1,0:T(8,128)S(1)}, u32[]{:S(2)}, u32[]{:S(2)}) collective-permute-start(f32[4,24,128]{2,1,0:T(8,128)S(1)} %slice.426), channel_id=1, source_target_pairs={{0,8},{8,16},{16,24},{24,32},{32,40},{40,48},{48,56},{56,64},{64,7... | collective-permute-start | bytes 147464 | tf_op jit(solution)/shard_map/ppermute | solution.py:50
  100.4 1.3 slice_multiply_fusion
  101.7 5.5 %copy.46 = f32[1,4,4,6,4,32,4]{6,5,4,3,2,1,0:T(8,128)} copy(f32[1,4,4,6,4,32,4]{5,3,1,6,4,2,0:T(8,128)} %get-tuple-element.68) | data formatting | bytes 393216 | tf_op jit(solution)/shard_map/slice | solution.py:168
  107.2 6.5 %squeeze.6 = f32[16,24,128]{2,1,0:T(8,128)S(1)} reshape(f32[1,4,4,6,4,32,4]{6,5,4,3,2,1,0:T(8,128)} %copy.46) | data formatting | bytes 393216 | tf_op jit(solution)/shard_map/squeeze | solution.py:168
  115.4 1.3 collective-permute-start.1
  116.8 3.5 %collective-permute-done.1 = f32[4,24,128]{2,1,0:T(8,128)S(1)} collective-permute-done((f32[4,24,128]{2,1,0:T(8,128)S(1)}, f32[4,24,128]{2,1,0:T(8,128)S(1)}, u32[]{:S(2)}, u32[]{:S(2)}) %collective-permute-start.1) | collective-permute-done | bytes 49184 | tf_op jit(solution)/shard_map/ppermute | solution.py:53
  120.3 5.1 %collective-permute-start.2 = (f32[24,4,128]{2,1,0:T(4,128)S(1)}, f32[24,4,128]{2,1,0:T(4,128)S(1)}, u32[]{:S(2)}, u32[]{:S(2)}) collective-permute-start(f32[24,4,128]{2,1,0:T(4,128)S(1)} %get-tuple-element.81), channel_id=1, source_target_pairs={{0,1},{1,2},{2,3},{3,4},{4,5},{5,6},{6,7},{8,9},{9,10},{10,11},{11... | collective-permute-start | bytes 147464 | tf_op jit(solution)/shard_map/ppermute | solution.py:50
  125.4 1.9 collective-permute-start.3
  127.4 4.3 %copy.48 = f32[1,4,4,6,4,32,4]{6,5,4,3,2,1,0:T(8,128)} copy(f32[1,4,4,6,4,32,4]{5,3,1,6,4,2,0:T(8,128)S(1)} %get-tuple-element.67) | data formatting | bytes 393216 | tf_op jit(solution)/shard_map/mul | solution.py:167
  133.8 6.5 %mul.306 = f32[16,24,128]{2,1,0:T(8,128)S(1)} reshape(f32[1,4,4,6,4,32,4]{6,5,4,3,2,1,0:T(8,128)} %copy.48) | data formatting | bytes 393216 | tf_op jit(solution)/shard_map/mul | solution.py:167
  140.3 9.2 %pmin.28 = f32[]{:T(128)} all-reduce(f32[]{:T(128)} %fusion.85), channel_id=1, replica_groups=mesh['gx_0'=4,'gx_1'=4,'gy_0'=4,'gy_1'=2] {'gx_0'}, use_global_device_ids=true, to_apply=%region_11.12 | all-reduce | flops 1 | bytes 8 | tf_op jit(solution)/shard_map/pmin | solution.py:60
  149.6 6.5 %mul.308 = f32[1,16,24,128]{3,2,1,0:T(8,128)S(1)} reshape(f32[1,4,4,6,4,32,4]{6,5,4,3,2,1,0:T(8,128)} %copy.48) | data formatting | bytes 393216 | tf_op jit(solution)/shard_map/mul | solution.py:167
  156.1 9.6 %pmin.29 = f32[]{:T(128)} all-reduce(f32[]{:T(128)} %pmin.28), channel_id=1, replica_groups=mesh['gx_0'=4,'gx_1'=4,'gy_0'=4,'gy_1'=2] {'gx_1'}, use_global_device_ids=true, to_apply=%region_12.13 | all-reduce | flops 1 | bytes 8 | tf_op jit(solution)/shard_map/pmin | solution.py:60
  166.4 1.3 collective-permute-start.4
  167.7 1.3 collective-permute-start.5
  169.0 8.8 %pmin.30 = f32[]{:T(128)} all-reduce(f32[]{:T(128)} %pmin.29), channel_id=1, replica_groups=mesh['gx_0'=4,'gx_1'=4,'gy_0'=4,'gy_1'=2] {'gy_0'}, use_global_device_ids=true, to_apply=%region_13.14 | all-reduce | flops 1 | bytes 8 | tf_op jit(solution)/shard_map/pmin | solution.py:60
  178.5 8.1 %collective-permute-start.6 = (f32[2,24,4,128]{3,2,1,0:T(4,128)}, f32[2,24,4,128]{3,2,1,0:T(4,128)}, u32[]{:S(2)}, u32[]{:S(2)}) collective-permute-start(f32[2,24,4,128]{3,2,1,0:T(4,128)} %get-tuple-element.73), channel_id=1, source_target_pairs={{0,1},{1,2},{2,3},{3,4},{4,5},{5,6},{6,7},{8,9},{9,10},{10,11},{11... | collective-permute-start | bytes 294920 | tf_op jit(solution)/shard_map/ppermute | solution.py:50
  186.6 2.9 collective-permute-start.7
  189.6 3.3 %pmin.31 = f32[]{:T(128)} all-reduce(f32[]{:T(128)} %pmin.30), channel_id=1, replica_groups=mesh['gx_0'=4,'gx_1'=4,'gy_0'=4,'gy_1'=2] {'gy_1'}, use_global_device_ids=true, to_apply=%region_14.15 | all-reduce | flops 1 | bytes 8 | tf_op jit(solution)/shard_map/pmin | solution.py:60
  197.3 4.3 %collective-permute-start.8 = (f32[1,24,128]{2,1,0:T(8,128)S(1)}, f32[1,24,128]{2,1,0:T(8,128)S(1)}, u32[]{:S(2)}, u32[]{:S(2)}) collective-permute-start(f32[1,24,128]{2,1,0:T(8,128)S(1)} %get-tuple-element.85), channel_id=1, source_target_pairs={{0,8},{8,16},{16,24},{24,32},{32,40},{40,48},{48,56},{56,64},{64,7... | collective-permute-start | bytes 36872 | tf_op jit(solution)/shard_map/ppermute | solution.py:50
  201.6 1.3 collective-permute-start.9
  202.9 3.1 collective-permute-done.9
  206.1 4.1 %collective-permute-start.10 = (f32[18,1,128]{2,1,0:T(1,128)S(1)}, f32[18,1,128]{2,1,0:T(1,128)S(1)}, u32[]{:S(2)}, u32[]{:S(2)}) collective-permute-start(f32[18,1,128]{2,1,0:T(1,128)S(1)} %get-tuple-element.83), channel_id=1, source_target_pairs={{0,1},{1,2},{2,3},{3,4},{4,5},{5,6},{6,7},{8,9},{9,10},{10,11},{11... | collective-permute-start | bytes 27656 | tf_op jit(solution)/shard_map/ppermute | solution.py:50
  210.1 1.9 collective-permute-start.11
  212.3 2.9 collective-permute-done.11
  218.2 16.5 %reshape.420 = f32[4,6,6,6,32,6]{5,4,0,3,2,1:T(8,128)} reshape(f32[4,6,6,6,192]{4,0,3,2,1:T(4,128)S(1)} %copy.51) | data formatting | bytes 1327104 | tf_op jit(solution)/shard_map/reshape | solution.py:106
  234.7 11.3 %copy.52 = f32[4,6,32,6,6,6]{2,1,0,5,4,3:T(8,128)S(1)} copy(f32[4,6,32,6,6,6]{5,2,0,4,3,1:T(8,128)} %bitcast.118) | data formatting | bytes 1327104 | tf_op jit(solution)/shard_map/transpose | solution.py:107
  246.0 2.0 reshape.460
  248.0 1.4 copy.53
  249.4 6.3 %scatter_custom_fusion.4 = f32[1536,216]{1,0:T(8,128)S(1)} fusion(s32[768]{0:T(1024)} %copy-done.3, f32[768,216]{1,0:T(8,128)S(1)} %copy.53, f32[]{:T(128)} %constant.201.clone.1), kind=kCustom, calls=%fused_computation.24 | custom fusion | bytes 1327616 | tf_op jit(solution)/shard_map/scatter | solution.py:244
  255.7 3.6 %reshape_transpose_transpose_reshape_reshape_reshape.16 = f32[128,1,2592]{2,1,0:T(1,128)} reshape(f32[1536,216]{1,0:T(8,128)S(1)} %scatter_custom_fusion.4) | data formatting | bytes 2654208 | tf_op jit(solution)/shard_map/reshape;transpose;transpose;reshape;reshape;reshape | solution.py:39
  259.3 11.2 %all-to-all-start.3 = ((f32[128,1,2592]{2,1,0:T(1,128)}), f32[128,1,2592]{2,1,0:T(1,128)S(1)}, u32[]{:S(2)}, u32[]{:S(2)}) async-start(f32[128,1,2592]{2,1,0:T(1,128)} %reshape_transpose_transpose_reshape_reshape_reshape.16), calls=%async_computation.3 | async-start | bytes 2752512 | tf_op jit(solution)/shard_map/all_to_all | solution.py:40
  271.5 21.7 %all-to-all-done.3 = f32[128,1,2592]{2,1,0:T(1,128)S(1)} async-done(((f32[128,1,2592]{2,1,0:T(1,128)}), f32[128,1,2592]{2,1,0:T(1,128)S(1)}, u32[]{:S(2)}, u32[]{:S(2)}) %all-to-all-start.3) | async-done | bytes 1327136 | tf_op jit(solution)/shard_map/all_to_all | solution.py:40
  293.3 2.1 reshape.468
  295.4 7.6 %scatter_custom_fusion.5 = f32[768,216]{1,0:T(8,128)S(1)} fusion(s32[1536]{0:T(1024)S(1)} %fusion.100, f32[1536,216]{1,0:T(8,128)} %reshape.468, f32[]{:T(128)} %constant.201.clone.1), kind=kCustom, calls=%fused_computation.59 | custom fusion | bytes 664064 | tf_op jit(solution)/shard_map/scatter | solution.py:256
  303.0 19.2 %convert_multiply_fusion = f32[768,4096]{1,0:T(8,128)} fusion(bf16[768,4096]{1,0:T(8,128)(2,1)} %param.16, bf16[768,4096]{1,0:T(8,128)(2,1)} %param.15, f32[768,216]{1,0:T(8,128)S(1)} %scatter_custom_fusion.5, f32[216,4096]{1,0:T(8,128)} %constant.228.clone, s32[4096]{0:T(1024)S(1)} %add_select_fusion, s32[768]{0:T(1024)S(1)} %copy-done.9), kind=kOutput, calls=%fused_computation.6 | convolution fusion | flops 8182038528 | bytes 29387776 | tf_op jit(solution)/shard_map/dot_general | solution.py:258
  (121 shorter events, 20.6 us)
Async XLA Ops:
  0.0 19.8 %copy-start.1 = (s32[768]{0:T(1024)S(1)}, s32[768]{0:T(1024)}, u32[]{:S(2)}) copy-start(s32[768]{0:T(1024)} %param.19) | copy-start | bytes 9220
  1.2 28.1 %slice-start = ((s8[6291456]{0:T(1024)(128)(4,1)}), s8[2097152]{0:T(1024)(128)(4,1)S(1)}, s32[]{:S(2)}) async-start(s8[6291456]{0:T(1024)(128)(4,1)} %bitcast.121), calls=%async_computation.4 | async-start | bytes 4194304
  1.2 28.1 %copy-start.8 = (s32[768]{0:T(1024)S(1)}, s32[768]{0:T(1024)}, u32[]{:S(2)}) copy-start(s32[768]{0:T(1024)} %param.17) | copy-start | bytes 9220
  6.5 48.8 %all-to-all-start.1 = ((s32[128,1,12]{2,1,0:T(1,128)}), s32[128,1,12]{2,1,0:T(1,128)S(1)}, u32[]{:S(2)}, u32[]{:S(2)}) async-start(s32[128,1,12]{2,1,0:T(1,128)} %bitcast.14), calls=%async_computation.1 | async-start | bytes 131072 | tf_op jit(solution)/shard_map/all_to_all | solution.py:40
  18.2 46.8 %copy-start.4 = (pred[24]{0:T(512)(128)(4,1)}, pred[24]{0:T(512)(128)(4,1)S(1)}, u32[]{:S(2)}) copy-start(pred[24]{0:T(512)(128)(4,1)S(1)} %compare_and_fusion.1) | copy-start | bytes 76
  19.3 10.0 %copy-start = (f32[4096,64]{1,0:T(8,128)S(1)}, f32[4096,64]{1,0:T(8,128)}, u32[]{:S(2)}) copy-start(f32[4096,64]{1,0:T(8,128)} %constant.227.clone) | copy-start | bytes 3145732
  19.8 26.3 %copy-start.3 = (s32[768]{0:T(1024)}, s32[768]{0:T(1024)S(1)}, u32[]{:S(2)}) copy-start(s32[768]{0:T(1024)S(1)} %get-tuple-element.92) | copy-start | bytes 9220
  19.8 9.5 %slice-start.1 = ((s8[6291456]{0:T(1024)(128)(4,1)}), s8[4194304]{0:T(1024)(128)(4,1)S(1)}, s32[]{:S(2)}) async-start(s8[6291456]{0:T(1024)(128)(4,1)} %bitcast.121), calls=%async_computation.5 | async-start | bytes 8388608
  45.9 19.9 %copy-start.6 = (pred[32]{0:T(512)(128)(4,1)}, pred[32]{0:T(512)(128)(4,1)S(1)}, u32[]{:S(2)}) copy-start(pred[32]{0:T(512)(128)(4,1)S(1)} %compare_and_fusion) | copy-start | bytes 100
  55.3 26.1 %all-to-all-start.2 = ((f32[128,1,1536]{2,1,0:T(1,128)}), f32[128,1,1536]{2,1,0:T(1,128)S(1)}, u32[]{:S(2)}, u32[]{:S(2)}) async-start(f32[128,1,1536]{2,1,0:T(1,128)} %bitcast.20), calls=%async_computation.2 | async-start | bytes 1572864 | tf_op jit(solution)/shard_map/all_to_all | solution.py:40
  81.4 177.9 %all-to-all-start = ((s32[128,1,12]{2,1,0:T(1,128)}), s32[128,1,12]{2,1,0:T(1,128)}, u32[]{:S(2)}, u32[]{:S(2)}) async-start(s32[128,1,12]{2,1,0:T(1,128)} %bitcast.4), calls=%async_computation | async-start | bytes 131072 | tf_op jit(solution)/shard_map/all_to_all | solution.py:40
  97.1 19.7 %collective-permute-start = (f32[4,24,128]{2,1,0:T(8,128)S(1)}, f32[4,24,128]{2,1,0:T(8,128)S(1)}, u32[]{:S(2)}, u32[]{:S(2)}) collective-permute-start(f32[4,24,128]{2,1,0:T(8,128)S(1)} %slice.426), channel_id=1, source_target_pairs={{0,8},{8,16},{16,24},{24,32},{32,40},{40,48},{48,56},{56,64},{64,7... | collective-permute-start | bytes 147464 | tf_op jit(solution)/shard_map/ppermute | solution.py:50
  107.2 20.1 %copy-start.5 = (pred[24]{0:T(512)(128)(4,1)S(1)}, pred[24]{0:T(512)(128)(4,1)}, u32[]{:S(2)}) copy-start(pred[24]{0:T(512)(128)(4,1)} %copy-done.4) | copy-start | bytes 76
  107.2 20.1 %copy-start.7 = (pred[32]{0:T(512)(128)(4,1)S(1)}, pred[32]{0:T(512)(128)(4,1)}, u32[]{:S(2)}) copy-start(pred[32]{0:T(512)(128)(4,1)} %copy-done.6) | copy-start | bytes 100
  114.3 17.8 %copy-start.2 = (pred[22,30]{1,0:T(8,128)(4,1)S(1)}, pred[22,30]{1,0:T(8,128)(4,1)}, u32[]{:S(2)}) copy-start(pred[22,30]{1,0:T(8,128)(4,1)} %get-tuple-element.99) | copy-start | bytes 1984
  115.4 4.8 %collective-permute-start.1 = (f32[4,24,128]{2,1,0:T(8,128)S(1)}, f32[4,24,128]{2,1,0:T(8,128)S(1)}, u32[]{:S(2)}, u32[]{:S(2)}) collective-permute-start(f32[4,24,128]{2,1,0:T(8,128)S(1)} %slice.429), channel_id=1, source_target_pairs={{8,0},{16,8},{24,16},{32,24},{40,32},{48,40},{56,48},{64,56},{72,6... | collective-permute-start | bytes 147464 | tf_op jit(solution)/shard_map/ppermute | solution.py:53
  120.3 11.4 %collective-permute-start.2 = (f32[24,4,128]{2,1,0:T(4,128)S(1)}, f32[24,4,128]{2,1,0:T(4,128)S(1)}, u32[]{:S(2)}, u32[]{:S(2)}) collective-permute-start(f32[24,4,128]{2,1,0:T(4,128)S(1)} %get-tuple-element.81), channel_id=1, source_target_pairs={{0,1},{1,2},{2,3},{3,4},{4,5},{5,6},{6,7},{8,9},{9,10},{10,11},{11... | collective-permute-start | bytes 147464 | tf_op jit(solution)/shard_map/ppermute | solution.py:50
  125.4 6.3 %collective-permute-start.3 = (f32[24,4,128]{2,1,0:T(4,128)S(1)}, f32[24,4,128]{2,1,0:T(4,128)S(1)}, u32[]{:S(2)}, u32[]{:S(2)}) collective-permute-start(f32[24,4,128]{2,1,0:T(4,128)S(1)} %get-tuple-element.82), channel_id=1, source_target_pairs={{1,0},{2,1},{3,2},{4,3},{5,4},{6,5},{7,6},{9,8},{10,9},{11,10},{12... | collective-permute-start | bytes 147464 | tf_op jit(solution)/shard_map/ppermute | solution.py:53
  166.4 11.4 %collective-permute-start.4 = (f32[2,4,24,128]{3,2,1,0:T(8,128)}, f32[2,4,24,128]{3,2,1,0:T(8,128)S(1)}, u32[]{:S(2)}, u32[]{:S(2)}) collective-permute-start(f32[2,4,24,128]{3,2,1,0:T(8,128)} %get-tuple-element.75), channel_id=1, source_target_pairs={{0,8},{8,16},{16,24},{24,32},{32,40},{40,48},{48,56},{56,64},{64,7... | collective-permute-start | bytes 294920 | tf_op jit(solution)/shard_map/ppermute | solution.py:50
  167.7 10.1 %collective-permute-start.5 = (f32[2,4,24,128]{3,2,1,0:T(8,128)}, f32[2,4,24,128]{3,2,1,0:T(8,128)S(1)}, u32[]{:S(2)}, u32[]{:S(2)}) collective-permute-start(f32[2,4,24,128]{3,2,1,0:T(8,128)} %get-tuple-element.76), channel_id=1, source_target_pairs={{8,0},{16,8},{24,16},{32,24},{40,32},{48,40},{56,48},{64,56},{72,6... | collective-permute-start | bytes 294920 | tf_op jit(solution)/shard_map/ppermute | solution.py:53
  178.5 15.3 %collective-permute-start.6 = (f32[2,24,4,128]{3,2,1,0:T(4,128)}, f32[2,24,4,128]{3,2,1,0:T(4,128)}, u32[]{:S(2)}, u32[]{:S(2)}) collective-permute-start(f32[2,24,4,128]{3,2,1,0:T(4,128)} %get-tuple-element.73), channel_id=1, source_target_pairs={{0,1},{1,2},{2,3},{3,4},{4,5},{5,6},{6,7},{8,9},{9,10},{10,11},{11... | collective-permute-start | bytes 294920 | tf_op jit(solution)/shard_map/ppermute | solution.py:50
  186.6 7.3 %collective-permute-start.7 = (f32[2,24,4,128]{3,2,1,0:T(4,128)}, f32[2,24,4,128]{3,2,1,0:T(4,128)}, u32[]{:S(2)}, u32[]{:S(2)}) collective-permute-start(f32[2,24,4,128]{3,2,1,0:T(4,128)} %get-tuple-element.74), channel_id=1, source_target_pairs={{1,0},{2,1},{3,2},{4,3},{5,4},{6,5},{7,6},{9,8},{10,9},{11,10},{12... | collective-permute-start | bytes 294920 | tf_op jit(solution)/shard_map/ppermute | solution.py:53
  197.3 5.6 %collective-permute-start.8 = (f32[1,24,128]{2,1,0:T(8,128)S(1)}, f32[1,24,128]{2,1,0:T(8,128)S(1)}, u32[]{:S(2)}, u32[]{:S(2)}) collective-permute-start(f32[1,24,128]{2,1,0:T(8,128)S(1)} %get-tuple-element.85), channel_id=1, source_target_pairs={{0,8},{8,16},{16,24},{24,32},{32,40},{40,48},{48,56},{56,64},{64,7... | collective-permute-start | bytes 36872 | tf_op jit(solution)/shard_map/ppermute | solution.py:50
  201.6 4.4 %collective-permute-start.9 = (f32[1,24,128]{2,1,0:T(8,128)S(1)}, f32[1,24,128]{2,1,0:T(8,128)S(1)}, u32[]{:S(2)}, u32[]{:S(2)}) collective-permute-start(f32[1,24,128]{2,1,0:T(8,128)S(1)} %get-tuple-element.86), channel_id=1, source_target_pairs={{8,0},{16,8},{24,16},{32,24},{40,32},{48,40},{56,48},{64,56},{72,6... | collective-permute-start | bytes 36872 | tf_op jit(solution)/shard_map/ppermute | solution.py:53
  206.1 6.2 %collective-permute-start.10 = (f32[18,1,128]{2,1,0:T(1,128)S(1)}, f32[18,1,128]{2,1,0:T(1,128)S(1)}, u32[]{:S(2)}, u32[]{:S(2)}) collective-permute-start(f32[18,1,128]{2,1,0:T(1,128)S(1)} %get-tuple-element.83), channel_id=1, source_target_pairs={{0,1},{1,2},{2,3},{3,4},{4,5},{5,6},{6,7},{8,9},{9,10},{10,11},{11... | collective-permute-start | bytes 27656 | tf_op jit(solution)/shard_map/ppermute | solution.py:50
  210.1 5.0 %collective-permute-start.11 = (f32[18,1,128]{2,1,0:T(1,128)S(1)}, f32[18,1,128]{2,1,0:T(1,128)S(1)}, u32[]{:S(2)}, u32[]{:S(2)}) collective-permute-start(f32[18,1,128]{2,1,0:T(1,128)S(1)} %get-tuple-element.84), channel_id=1, source_target_pairs={{1,0},{2,1},{3,2},{4,3},{5,4},{6,5},{7,6},{9,8},{10,9},{11,10},{12... | collective-permute-start | bytes 27656 | tf_op jit(solution)/shard_map/ppermute | solution.py:53
  255.7 47.3 %copy-start.9 = (s32[768]{0:T(1024)S(1)}, s32[768]{0:T(1024)}, u32[]{:S(2)}) copy-start(s32[768]{0:T(1024)} %param.17) | copy-start | bytes 9220
  259.3 33.9 %all-to-all-start.3 = ((f32[128,1,2592]{2,1,0:T(1,128)}), f32[128,1,2592]{2,1,0:T(1,128)S(1)}, u32[]{:S(2)}, u32[]{:S(2)}) async-start(f32[128,1,2592]{2,1,0:T(1,128)} %reshape_transpose_transpose_reshape_reshape_reshape.16), calls=%async_computation.3 | async-start | bytes 2752512 | tf_op jit(solution)/shard_map/all_to_all | solution.py:40
where the time goes:
time: 326 us; the launch traced here: 323 us
  local copies, waits for them, and re-layouts  109 us (33%)
  starting transfers between devices  75 us (23%)
  matrix products  47.4 us (15%)
  waiting for transfers between devices  46.6 us (14%)
  blocking collectives  30.9 us (9%)
  other arithmetic  11.8 us (4%)
    all_to_all x4, starting transfers between devices, one_exchange(): lax.all_to_all(blocks, axis, split_axis=0, concat_axis=0, tiled=True)  38.3 us
    all_to_all x4, waiting for transfers between devices, one_exchange(): lax.all_to_all(blocks, axis, split_axis=0, concat_axis=0, tiled=True)  37.1 us
    pmin x4, blocking collectives, over_axes(): shard = lax.pmin(shard, axis)  30.9 us
    ppermute x6, starting transfers between devices, with_halo(): lax.ppermute(lax.slice_in_dim(block, block.shape[dim] - width, None, axis...  26.1 us
    dot_general x1, matrix products, on_device(): fine_field = jnp.dot(by_slot, spread_table(), precision=EXACT_DOT)  19.2 us
    mul x3, local copies, waits for them, and re-layouts, on_device(): source = 4.0 * coarse_grid[0]  17.3 us
    dot_general x1, matrix products, on_device(): jnp.dot(emission, averaging, precision=EXACT_DOT)  16.6 us
    reshape x1, local copies, waits for them, and re-layouts, cut_windows(): along_x.reshape(blocks_x, blocks_y, border, border, blocks_z, border)  16.5 us
  transfers between devices with their start and end apart: 16, of which 5 were waited for; matrix products, arithmetic and copies ran while one was open for 41% of the time, Pallas kernels for 0%

commit v1 on v0

v1 whole, which is shorter than its diff:
```python
import functools

import jax
import jax.numpy as jnp
import numpy as np
from jax import lax
from jax.experimental import pallas as pl
from jax.experimental.pallas import tpu as pltpu
from jax.sharding import PartitionSpec as P

MESH = pl.DeviceIdType.MESH
F32 = jnp.float32
BF16 = jnp.bfloat16
BX, BY, BZ = 4, 6, 32
CX, CY = 16, 24
SLOTS = 768
NDEV = 128
CAP = 12
PAD = 16
ROWS = 128
XH, YH = 6, 8
EX, EY = CX + 2 * XH, CY + 2 * YH


def average_table():
    table = np.zeros((4, 2, 2, 8, 16, 4, 2, 4, 4), np.float32)
    for i in range(4):
        for bh in range(2):
            for f in range(2):
                for b in range(8):
                    for c in range(16):
                        weight = 1.0 / 16.0 if f == 0 else 1.0 / 64.0
                        table[i, bh, f, b, c, c // 4, f, i, 2 * bh + b // 4] = weight
    return jnp.asarray(table.reshape(8, 256, 128), BF16)


def select_table():
    table = np.zeros((BY, 6, 128, 128), np.float32)
    for v in range(BY):
        for l in range(6):
            for i in range(3):
                for j in range(6):
                    table[v, l, i * 40 + 7 + 4 * v + j, i * 42 + j * 6 + l] = 1.0
    return jnp.asarray(table.reshape(BY, 768, 128), BF16)


def twice_table():
    table = np.zeros((2, 2, 128, 6, 2, 64), np.float32)
    for i in range(6):
        for jl in range(36):
            table[:, i // 3, (i % 3) * 42 + jl, i, :, jl] = 1.0
    return jnp.asarray(table.reshape(512, 768), BF16)


def line_weights():
    weights = np.zeros((16, 6))
    for a in range(16):
        position = (a + 0.5) / 4 + 0.5
        low = int(np.floor(position))
        weights[a, low] += 1.0 - (position - low)
        weights[a, low + 1] += position - low
    return weights


def plane_table():
    w = line_weights()
    plane = np.zeros((2, 64, 256))
    plane[:, :36] = np.kron(w, w).T
    return jnp.asarray(plane.reshape(128, 256), BF16)


def halves(x):
    high = x.astype(BF16)
    return high, (x - high.astype(F32)).astype(BF16)


def dot(a, b):
    return jnp.dot(a, b, preferred_element_type=F32)


def column(row):
    return jnp.broadcast_to(row, (128, 128)).T


def lanes(shape):
    return lax.broadcasted_iota(jnp.int32, shape, len(shape) - 1)


def place(index):
    return (index // 8, index % 8)


def greet_all():
    barrier = pltpu.get_barrier_semaphore()
    gx, gy = lax.axis_index("gx"), lax.axis_index("gy")
    for p in range(16):
        px = (gx + p) % 16
        for t in range(8):
            if p or t:
                pl.semaphore_signal(
                    barrier, inc=1, device_id=(px, (gy + t) % 8), device_id_type=MESH
                )
    return barrier


def peers():
    gx, gy = lax.axis_index("gx"), lax.axis_index("gy")
    x, y, z, c = gx // 4, gx % 4, gy // 2, gy % 2
    xs = [((x + t) % 4) * 4 for t in range(4)]
    ys = [(y + t) % 4 for t in range(4)]
    zs = [((z + t) % 4) * 2 for t in range(4)]
    cs = [(c + t) % 2 for t in range(2)]
    for p in range(1, NDEV):
        q = p * 45 % NDEV
        yield xs[q // 32] + ys[q // 8 % 4], zs[q // 2 % 4] + cs[q % 2]


def rank_row(owner, key):
    owner_c = [column(owner[:, i * 128 : i * 128 + 128]) for i in range(6)]
    key_c = [column(key[:, i * 128 : i * 128 + 128]) for i in range(6)]
    out = []
    for j in range(6):
        ro, rk = owner[:, j * 128 : j * 128 + 128], key[:, j * 128 : j * 128 + 128]
        total = jnp.zeros((128, 128), F32)
        for i in range(6):
            total += jnp.where((owner_c[i] == ro) & (key_c[i] < rk), 1.0, 0.0)
        out.append(jnp.sum(total, axis=0, keepdims=True))
    return jnp.concatenate(out, axis=1)


def index_kernel(p2t_ref, t2p_ref, target_ref, source_ref):
    box = p2t_ref[...].astype(F32)
    owner = jnp.floor((box + 0.5) * (1.0 / SLOTS))
    slot = lanes((1, SLOTS)).astype(F32)
    target_ref[...] = owner * PAD + rank_row(owner, slot)
    slot = t2p_ref[...].astype(F32)
    home = jnp.floor((slot + 0.5) * (1.0 / SLOTS))
    source_ref[...] = home * PAD + rank_row(home, slot)


def one_hot(row, start, count):
    index = lax.broadcasted_iota(jnp.int32, (count, row.shape[1]), 0) + start
    return jnp.where(index.astype(F32) == row, 1.0, 0.0).astype(BF16)


def restrict_kernel(t_ref, k_ref, depth_ref, target_ref, table_ref, out_ref, held):
    step = pl.program_id(0)
    depth = column(depth_ref[...].astype(F32))
    layer = (lanes((128, 128)) % 16).astype(F32)
    mask = jnp.where(layer < depth, 1.0, 0.0)
    total = jnp.zeros((ROWS, 128), F32)
    for i in range(4):
        for bh in range(2):
            glow = absorb = None
            for a in range(4):
                at = (4 * i + a) * 256 + bh * 128
                t = t_ref[:, at : at + 128].astype(F32)
                k = k_ref[:, at : at + 128].astype(F32)
                square = t * t
                term = k * (square * square)
                glow = term if glow is None else glow + term
                absorb = k if absorb is None else absorb + k
            high, low = halves(jnp.concatenate([glow * mask, absorb], axis=1))
            table = table_ref[2 * i + bh]
            total += dot(high, table) + dot(low, table)
    held[pl.ds(pl.multiple_of(step * ROWS, ROWS), ROWS), :] = total

    @pl.when(step == SLOTS // ROWS - 1)
    def _():
        high, low = halves(held[...])
        target = target_ref[...]

        @pl.loop(0, NDEV // 16)
        def _(chunk):
            hot = one_hot(target, chunk * 256, 256)
            block = (dot(hot, high) + dot(hot, low)).reshape(16, PAD, 128)
            out_ref[pl.ds(chunk * 16, 16)] = block[:, :CAP]


def exchange_kernel(x_ref, o_ref, send_sem, recv_sem, local_sem):
    gx, gy = lax.axis_index("gx"), lax.axis_index("gy")
    me = gx * 8 + gy
    barrier = greet_all()
    local = pltpu.make_async_copy(x_ref.at[me], o_ref.at[me], local_sem)
    local.start()
    pl.semaphore_wait(barrier, NDEV - 1)
    send_all(x_ref, o_ref, send_sem, recv_sem)
    local.wait()
    wait_all(x_ref, o_ref, send_sem, recv_sem)


def send_all(x_ref, o_ref, send_sem, recv_sem):
    me = lax.axis_index("gx") * 8 + lax.axis_index("gy")
    for px, py in peers():
        pltpu.make_async_remote_copy(
            src_ref=x_ref.at[px * 8 + py],
            dst_ref=o_ref.at[me],
            send_sem=send_sem,
            recv_sem=recv_sem,
            device_id=(px, py),
            device_id_type=MESH,
        ).start()


def wait_all(x_ref, o_ref, send_sem, recv_sem):
    others = pl.ds(0, NDEV - 1)
    pltpu.make_async_copy(x_ref.at[others], o_ref.at[others], recv_sem).wait()
    pltpu.make_async_copy(x_ref.at[others], o_ref.at[others], send_sem).wait()


def padded_rows(value):
    n = value.shape[0]
    zeros = jnp.zeros((n, PAD - CAP, 128), F32)
    return jnp.concatenate([value, zeros], axis=1).reshape(n * PAD, 128)


def assemble_kernel(arrived_ref, source_ref, grid_ref):
    source = source_ref[...]

    def chunk(c, total):
        rows = padded_rows(arrived_ref[pl.ds(c * 16, 16)])
        high, low = halves(jnp.concatenate([rows[:128].T, rows[128:].T], axis=1))
        hot = one_hot(source, c * 256, 256)
        return total + dot(high, hot) + dot(low, hot)

    total = lax.fori_loop(0, NDEV // 16, chunk, jnp.zeros((128, SLOTS), F32))
    group = lanes((32, 128)) // 32
    for v in range(BY):
        for u in range(BX):
            out = None
            for l in range(4):
                part = total[l * 32 : l * 32 + 32, v * 128 : v * 128 + 128]
                part = pltpu.roll(part, (l - u) * 32 % 128, 1)
                out = part if out is None else jnp.where(group == l, part, out)
            for f in range(2):
                for i in range(4):
                    at = (f * 4 + i) * 4
                    grid_ref[f, 4 * u + i, 4 * v : 4 * v + 4, :] = out[at : at + 4]


def halo_copies(grid_ref, hx_ref, hy_ref, hc_ref, send_sem, recv_sem):
    gx, gy = lax.axis_index("gx"), lax.axis_index("gy")
    up_x, down_x = (gx + 1) % 16, (gx + 15) % 16
    up_y, down_y = (gy + 1) % 8, (gy + 7) % 8
    last_x, first_x = pl.ds(CX - XH, XH), pl.ds(0, XH)
    last_y, first_y = pl.ds(CY - YH, YH), pl.ds(0, YH)
    every = slice(None)
    plan = [
        (grid_ref.at[:, last_x], hx_ref.at[0], (up_x, gy)),
        (grid_ref.at[:, first_x], hx_ref.at[1], (down_x, gy)),
        (grid_ref.at[:, :, last_y], hy_ref.at[0], (gx, up_y)),
        (grid_ref.at[:, :, first_y], hy_ref.at[1], (gx, down_y)),
        (grid_ref.at[:, last_x, last_y], hc_ref.at[0], (up_x, up_y)),
        (grid_ref.at[:, last_x, first_y], hc_ref.at[1], (up_x, down_y)),
        (grid_ref.at[:, first_x, last_y], hc_ref.at[2], (down_x, up_y)),
        (grid_ref.at[:, first_x, first_y], hc_ref.at[3], (down_x, down_y)),
    ]
    return [
        pltpu.make_async_remote_copy(
            src_ref=src,
            dst_ref=dst,
            send_sem=send_sem.at[n],
            recv_sem=recv_sem.at[n],
            device_id=who,
            device_id_type=MESH,
        )
        for n, (src, dst, who) in enumerate(plan)
    ]


def halo_kernel(grid_ref, hx_ref, hy_ref, hc_ref, send_sem, recv_sem):
    gx, gy = lax.axis_index("gx"), lax.axis_index("gy")
    barrier = pltpu.get_barrier_semaphore()
    for dx in (1, 0, 15):
        for dy in (1, 0, 7):
            if dx or dy:
                who = ((gx + dx) % 16, (gy + dy) % 8)
                pl.semaphore_signal(barrier, inc=1, device_id=who, device_id_type=MESH)
    pl.semaphore_wait(barrier, 8)
    copies = halo_copies(grid_ref, hx_ref, hy_ref, hc_ref, send_sem, recv_sem)
    for copy in copies:
        copy.start()
    for copy in copies:
        copy.wait()


def z_lower(v):
    lane = lanes(v.shape)
    return jnp.where(lane < 32, pltpu.roll(v, 33, 1), pltpu.roll(v, 32, 1))


def z_upper(v):
    lane = lanes(v.shape)
    return jnp.where(lane >= 96, pltpu.roll(v, 95, 1), pltpu.roll(v, 96, 1))


def face(a, b):
    return (2.0 / 3.0) / (a + b)


def solve_kernel(
    grid_ref, hx_ref, hy_ref, hc_ref, a_ref, b_ref, c_ref, low_ref, ext, w, v
):
    gx, gy = lax.axis_index("gx"), lax.axis_index("gy")
    own_x, own_y = pl.ds(XH, CX), pl.ds(YH, CY)
    for f in range(2):
        ext[f, own_x, own_y] = grid_ref[f]
        for side, at in ((0, 0), (1, XH + CX)):
            ext[f, pl.ds(at, XH), own_y] = hx_ref[side, f]
        for side, at in ((0, 0), (1, YH + CY)):
            ext[f, own_x, pl.ds(at, YH)] = hy_ref[side, f]
        for n, (atx, aty) in enumerate(
            ((0, 0), (0, YH + CY), (XH + CX, 0), (XH + CX, YH + CY))
        ):
            ext[f, pl.ds(atx, XH), pl.ds(aty, YH)] = hc_ref[n, f]
    shape = (EY, 128)
    row = lax.broadcasted_iota(jnp.int32, shape, 0)
    lane = lanes(shape)
    y_at = gy * CY + row - YH
    has_ym, has_yp = y_at >= 1, y_at <= 8 * CY - 2
    has_zm, has_zp = lane != 0, lane != 127

    def coefficients(x, low):
        x_at = gx * CX + x - XH
        k = ext[1, x]
        has_xm = jnp.broadcast_to(x_at, shape) >= 1
        has_xp = jnp.broadcast_to(x_at, shape) <= 16 * CX - 2
        near = (
            (has_xm, ext[1, x - 1]),
            (has_xp, ext[1, x + 1]),
            (has_ym, pltpu.roll(k, 1, 0)),
            (has_yp, pltpu.roll(k, EY - 1, 0)),
            (has_zm, z_lower(k)),
            (has_zp, z_upper(k)),
        )
        faces = [face(k, jnp.where(has, other, k)) for has, other in near]
        diagonal = k
        for c in faces:
            diagonal = diagonal + c
        inverse = 1.0 / diagonal
        for n, c in enumerate(faces):
            w[n, x] = jnp.where(near[n][0], c * inverse, 0.0)
        v[0, x] = inverse * ext[0, x]
        own = jnp.broadcast_to((x >= XH) & (x < XH + CX), shape)
        return jnp.minimum(low, jnp.where(own, k * inverse, 1.0))

    low = lax.fori_loop(1, EX - 1, coefficients, jnp.ones(shape, F32))
    low_ref[...] = jnp.broadcast_to(
        jnp.min(jnp.min(low[YH : YH + CY], axis=0, keepdims=True), axis=1, keepdims=True),
        low_ref.shape,
    )

    for n in range(4):

        def apply(x, _, n=n):
            mid = v[n, x]
            v[n + 1, x] = (
                w[0, x] * v[n, x - 1]
                + w[1, x] * v[n, x + 1]
                + w[2, x] * pltpu.roll(mid, 1, 0)
                + w[3, x] * pltpu.roll(mid, EY - 1, 0)
                + w[4, x] * z_lower(mid)
                + w[5, x] * z_upper(mid)
            )
            return 0

        lax.fori_loop(2 + n, EX - 2 - n, apply, 0)
    for x in range(CX + 2):
        at = x + XH - 1
        a_ref[x] = v[0, at]
        b_ref[x] = v[1, at] + v[2, at]
        c_ref[x] = v[3, at] + v[4, at]


def lowest_kernel(low_ref, o_ref, send_sem, recv_sem, local_sem):
    me = lax.axis_index("gx") * 8 + lax.axis_index("gy")
    barrier = greet_all()
    local = pltpu.make_async_copy(low_ref, o_ref.at[me], local_sem)
    local.start()
    pl.semaphore_wait(barrier, NDEV - 1)
    for px, py in peers():
        pltpu.make_async_remote_copy(
            src_ref=low_ref,
            dst_ref=o_ref.at[me],
            send_sem=send_sem,
            recv_sem=recv_sem,
            device_id=(px, py),
            device_id_type=MESH,
        ).start()
    local.wait()
    others = pl.ds(0, NDEV - 1)
    pltpu.make_async_copy(o_ref.at[others], o_ref.at[others], recv_sem).wait()
    pltpu.make_async_copy(o_ref.at[others], o_ref.at[others], send_sem).wait()


def pack_kernel(
    a_ref, b_ref, c_ref, lows_ref, source_ref, table_ref, out_ref, inc, win
):
    gx, gy = lax.axis_index("gx"), lax.axis_index("gy")
    lowest = jnp.min(lows_ref[...], axis=0)
    delta = 1.0 - jnp.broadcast_to(lowest, (EY, 128))
    square = delta * delta
    scale = 1.0 / (16.0 - 20.0 * square + 5.0 * square * square)
    outer = 16.0 * scale
    inner = outer - 20.0 * square * scale
    row = lax.broadcasted_iota(jnp.int32, (EY, 128), 0)
    first_row = (row == YH - 1) & jnp.broadcast_to(gy == 0, (EY, 128))
    last_row = (row == YH + CY) & jnp.broadcast_to(gy == 7, (EY, 128))
    for x in range(CX + 2):
        value = a_ref[x] + inner * b_ref[x] + outer * c_ref[x]
        value = jnp.where(first_row, pltpu.roll(value, EY - 1, 0), value)
        inc[x] = jnp.where(last_row, pltpu.roll(value, 1, 0), value)
    inc[0] = jnp.where(jnp.broadcast_to(gx == 0, (EY, 128)), inc[1], inc[0])
    inc[CX + 1] = jnp.where(
        jnp.broadcast_to(gx == 15, (EY, 128)), inc[CX], inc[CX + 1]
    )
    edge = lax.broadcasted_iota(jnp.int32, (32, 128), 0)
    for h in range(2):
        pieces = [[] for _ in range(6)]
        for u in range(BX):
            stack = [inc[4 * u + 3 * h + i] for i in range(3)]
            stack = jnp.concatenate([*stack, jnp.zeros((8, 128), F32)], axis=0).T
            part = [stack[l * 32 : l * 32 + 32] for l in range(4)]
            pieces[0].append(jnp.where(edge == 0, part[0], pltpu.roll(part[3], 1, 0)))
            for l in range(4):
                pieces[l + 1].append(part[l])
            pieces[5].append(jnp.where(edge == 31, part[3], pltpu.roll(part[0], 31, 0)))
        rows = jnp.concatenate([jnp.concatenate(p, axis=0) for p in pieces], axis=1)
        high, low = halves(rows)
        for v in range(BY):
            table = table_ref[v]
            value = dot(high, table) + dot(low, table)
            top, rest = halves(value)
            win[0, v * 128 : v * 128 + 128, h * 128 : h * 128 + 128] = top
            win[1, v * 128 : v * 128 + 128, h * 128 : h * 128 + 128] = rest
    source = source_ref[...]

    @pl.loop(0, NDEV // 16)
    def _(chunk):
        hot = one_hot(source, chunk * 256, 256)
        block = dot(hot, win[0]) + dot(hot, win[1])
        for h in range(2):
            part = block[:, h * 128 : h * 128 + 128].reshape(16, PAD, 128)
            out_ref[pl.ds(chunk * 16, 16), h] = part[:, :CAP]


def prolong_kernel(
    back_ref, target_ref, t_ref, k_ref, depth_ref, twice_ref, plane_ref, out_ref, held
):
    step = pl.program_id(0)

    @pl.when(step == 0)
    def _():
        for h in range(2):
            high, low = halves(padded_rows(back_ref[:, h]))
            held[:, h * 128 : h * 128 + 128] = high
            held[:, 256 + h * 128 : 256 + h * 128 + 128] = low

    target = column(target_ref[...])
    hot = jnp.concatenate(
        [
            jnp.where((lanes((128, 128)) + c * 128).astype(F32) == target, 1.0, 0.0).astype(BF16)
            for c in range(PAD)
        ],
        axis=1,
    )
    mine = dot(hot, held[...]).astype(BF16)
    both = dot(mine, twice_ref[...])
    depth = column(depth_ref[...].astype(F32))
    lane = lanes((128, 128))
    mask = jnp.where((lane % 16).astype(F32) < depth, 4.0, 0.0)
    first = lane < 64
    weights = line_weights()
    plane = plane_ref[...]
    for a in range(16):
        low = int(np.flatnonzero(weights[a])[0])
        value = float(weights[a, low]) * both[:, low * 128 : low * 128 + 128] + float(
            weights[a, low + 1]
        ) * both[:, low * 128 + 128 : low * 128 + 256]
        rest = value - value.astype(BF16).astype(F32)
        fine = dot(jnp.where(first, value, rest).astype(BF16), plane)
        for b in range(2):
            at = a * 256 + b * 128
            t = t_ref[:, at : at + 128].astype(F32)
            k = k_ref[:, at : at + 128].astype(F32)
            square = t * t
            out_ref[:, at : at + 128] = k * (
                fine[:, b * 128 : b * 128 + 128] - mask * (square * square)
            )


VM = pl.BlockSpec(memory_space=pltpu.VMEM)
LIMIT = 60 * 1024 * 1024


def struct(*shape):
    return jax.ShapeDtypeStruct(shape, F32)


def call(kernel, out, n_in, scratch=(), collective=None, name=None):
    params = {"vmem_limit_bytes": LIMIT}
    if collective is not None:
        params.update(collective_id=collective, has_side_effects=True)
    several = isinstance(out, (list, tuple))
    return pl.pallas_call(
        kernel,
        out_shape=out,
        in_specs=[VM] * n_in,
        out_specs=[VM] * len(out) if several else VM,
        scratch_shapes=list(scratch),
        compiler_params=pltpu.CompilerParams(**params),
        name=name,
    )


def on_device(thermal_state, opacity_field, glowing_depth, position_to_tile, tile_to_position):
    dma = pltpu.SemaphoreType.DMA
    depth = glowing_depth.reshape(1, SLOTS)
    boxes = position_to_tile.reshape(1, SLOTS)
    places = tile_to_position.reshape(BX, BY, BZ).transpose(1, 0, 2).reshape(1, SLOTS)
    target, source = call(index_kernel, [struct(1, SLOTS), struct(1, SLOTS)], 2, name="index")(
        boxes, places
    )
    steps = SLOTS // ROWS
    wide = pl.BlockSpec((ROWS, 4096), lambda i: (i, 0))
    few = pl.BlockSpec((1, ROWS), lambda i: (0, i))
    outgoing = pl.pallas_call(
        restrict_kernel,
        out_shape=struct(NDEV, CAP, 128),
        grid=(steps,),
        in_specs=[wide, wide, few, VM, VM],
        out_specs=pl.BlockSpec((NDEV, CAP, 128), lambda i: (0, 0, 0)),
        scratch_shapes=[pltpu.VMEM((SLOTS, 128), F32)],
        compiler_params=pltpu.CompilerParams(vmem_limit_bytes=LIMIT),
        name="restrict",
    )(thermal_state, opacity_field, depth, target, average_table())
    arrived = call(
        exchange_kernel, struct(NDEV, CAP, 128), 1, [dma, dma, dma], 0, name="exchange"
    )(outgoing)
    grid = call(assemble_kernel, struct(2, CX, CY, 128), 2, name="assemble")(arrived, source)
    hx, hy, hc = call(
        halo_kernel,
        [struct(2, 2, XH, CY, 128), struct(2, 2, CX, YH, 128), struct(4, 2, XH, YH, 128)],
        1,
        [dma((8,)), dma((8,))],
        1,
        name="halo",
    )(grid)
    plane = struct(CX + 2, EY, 128)
    a, b, c, low = call(
        solve_kernel,
        [plane, plane, plane, struct(1, 128)],
        4,
        [
            pltpu.VMEM((2, EX, EY, 128), F32),
            pltpu.VMEM((6, EX, EY, 128), F32),
            pltpu.VMEM((5, EX, EY, 128), F32),
        ],
        name="solve",
    )(grid, hx, hy, hc)
    lows = call(lowest_kernel, struct(NDEV, 1, 128), 1, [dma, dma, dma], 2, name="lowest")(low)
    leaving = call(
        pack_kernel,
        struct(NDEV, 2, CAP, 128),
        6,
        [pltpu.VMEM((CX + 2, EY, 128), F32), pltpu.VMEM((2, SLOTS, 256), BF16)],
        name="pack",
    )(a, b, c, lows, source, select_table())
    back = call(
        exchange_kernel, struct(NDEV, 2, CAP, 128), 1, [dma, dma, dma], 3, name="return"
    )(leaving)
    return pl.pallas_call(
        prolong_kernel,
        out_shape=struct(SLOTS, 4096),
        grid=(steps,),
        in_specs=[VM, few, wide, wide, few, VM, VM],
        out_specs=wide,
        scratch_shapes=[pltpu.VMEM((NDEV * PAD, 512), BF16)],
        compiler_params=pltpu.CompilerParams(vmem_limit_bytes=LIMIT),
        name="prolong",
    )(back, target, thermal_state, opacity_field, depth, twice_table(), plane_table())


def solution(mesh):
    rows = P(("gx", "gy"), None)
    ints = P(("gx", "gy"))
    return jax.shard_map(
        on_device,
        mesh=mesh,
        in_specs=(rows, rows, ints, ints, ints),
        out_specs=rows,
        check_vma=False,
    )
```

time: 326 us -> 142 us (0.44)
  Pallas kernels: 0 us -> 137 us
  local copies, waits for them, and re-layouts: 109 us -> 3.98 us
  starting transfers between devices: 75 us -> 0 us
  matrix products: 47.4 us -> 0 us
  waiting for transfers between devices: 46.6 us -> 0 us
  blocking collectives: 30.9 us -> 0 us
  other arithmetic: 11.8 us -> 0 us
    pallas_call x0 -> x10, Pallas kernels: none -> 137 us  [the longest x1 29.4 us: on_device(): call(exchange_kernel, struct(NDEV, 2, CAP, 128), 1, [dma, dma, dma], 3, n...]
    dot_general x6 -> x0, matrix products: 47.4 us -> none  [the longest x1 19.2 us: on_device(): fine_field = jnp.dot(by_slot, spread_table(), precision=EXACT_DOT)]
    all_to_all x4 -> x0, starting transfers between devices: 38.3 us -> none  [one_exchange(): lax.all_to_all(blocks, axis, split_axis=0, concat_axis=0, tiled=True)]
    all_to_all x4 -> x0, waiting for transfers between devices: 37.1 us -> none  [one_exchange(): lax.all_to_all(blocks, axis, split_axis=0, concat_axis=0, tiled=True)]
    ppermute x12 -> x0, starting transfers between devices: 36.7 us -> none  [the longest x6 26.1 us: with_halo(): lax.ppermute(lax.slice_in_dim(block, block.shape[dim] - width, None, axis...]
    pmin x4 -> x0, blocking collectives: 30.9 us -> none  [over_axes(): shard = lax.pmin(shard, axis)]
    scatter x9 -> x0, local copies, waits for them, and re-layouts: 30.5 us -> none  [the longest x1 7.56 us: on_device(): jnp.zeros((stack_tiles, border ** 3), jnp.float32).at[slot_rows]]
    mul x3 -> x0, local copies, waits for them, and re-layouts: 17.3 us -> none  [on_device(): source = 4.0 * coarse_grid[0]]
  transfers between devices with their start and end apart: 16 -> 0, of which waited for: 5 -> 0; matrix products, arithmetic and copies ran while one was open for 41% -> 0% of each run, Pallas kernels for 0% -> 0%
where the time goes in v1:
time: 142 us; the launch traced here: 141 us
  Pallas kernels  137 us (96%)
  local copies, waits for them, and re-layouts  3.98 us (3%)
    pallas_call x1, Pallas kernels, on_device(): call(exchange_kernel, struct(NDEV, 2, CAP, 128), 1, [dma, dma, dma], 3, n...  29.4 us
    pallas_call x1, Pallas kernels, on_device(): call(exchange_kernel, struct(NDEV, CAP, 128), 1, [dma, dma, dma], 0, name...  24.3 us
    pallas_call x1, Pallas kernels, on_device(): pl.pallas_call(prolong_kernel, out_shape=struct(SLOTS, 4096), grid=(steps...  15.2 us
    pallas_call x1, Pallas kernels, on_device(): call(halo_kernel, [struct(2, 2, XH, CY, 128), struct(2, 2, CX, YH, 128),...  14 us
    pallas_call x1, Pallas kernels, on_device(): call(lowest_kernel, struct(NDEV, 1, 128), 1, [dma, dma, dma], 2, name='lo...  13.3 us
    pallas_call x1, Pallas kernels, on_device(): call(solve_kernel, [plane, plane, plane, struct(1, 128)], 4, [pltpu.VMEM(...  13.2 us
    pallas_call x1, Pallas kernels, on_device(): pl.pallas_call(restrict_kernel, out_shape=struct(NDEV, CAP, 128), grid=(s...  12.5 us
    pallas_call x1, Pallas kernels, on_device(): call(pack_kernel, struct(NDEV, 2, CAP, 128), 6, [pltpu.VMEM((CX + 2, EY,...  7.5 us

profile of v1, /device:TPU:1, one launch (start us, length us, event | category | flops | bytes accessed | tf_op | source)
XLA Modules:
  0.0 140.9 jit_solution(2073290330993838735)
XLA Ops:
  0.0 1.3 reshape.12.depth_ref
  1.3 1.3 reshape.13.p2t_ref
  2.5 0.8 reshape.14
  3.3 0.7 reshape.15.t2p_ref
  4.0 2.3 %index.1 = (f32[1,768]{1,0:T(1,128)}, f32[1,768]{1,0:T(1,128)}) custom-call(s32[1,768]{1,0:T(1,128)} %reshape.13.p2t_ref, s32[1,768]{1,0:T(1,128)} %reshape.15.t2p_ref), custom_call_target="tpu_custom_call" | custom-call | tf_op jit(solution)/shard_map/index/pallas_call | solution.py:521
  6.2 12.5 %restrict.1.x_ref = f32[128,12,128]{2,1,0:T(8,128)} custom-call(bf16[768,4096]{1,0:T(8,128)(2,1)} %t_ref.3, bf16[768,4096]{1,0:T(8,128)(2,1)} %k_ref.3, s32[1,768]{1,0:T(1,128)} %reshape.12.depth_ref, f32[1,768]{1,0:T(1,128)} %get-tuple-element.14.target_ref, bf16[8,256,128]{2,1,0:T(8,128)(2,1)} %constant.8.clone.table_ref), custom_call_target="tpu_custom_call" | custom-call | tf_op jit(solution)/shard_map/restrict/pallas_call | solution.py:527
  18.8 24.3 %exchange.1.arrived_ref = f32[128,12,128]{2,1,0:T(8,128)} custom-call(f32[128,12,128]{2,1,0:T(8,128)} %restrict.1.x_ref), custom_call_target="tpu_custom_call" | custom-call | tf_op jit(solution)/shard_map/exchange/pallas_call | solution.py:537
  43.0 5.2 %assemble.1.grid_ref = f32[2,16,24,128]{3,2,1,0:T(8,128)} custom-call(f32[128,12,128]{2,1,0:T(8,128)} %exchange.1.arrived_ref, f32[1,768]{1,0:T(1,128)} %get-tuple-element.15.source_ref), custom_call_target="tpu_custom_call" | custom-call | tf_op jit(solution)/shard_map/assemble/pallas_call | solution.py:540
  48.2 14.0 %halo.1 = (f32[2,2,6,24,128]{4,3,2,1,0:T(8,128)}, f32[2,2,16,8,128]{4,3,2,1,0:T(8,128)}, f32[4,2,6,8,128]{4,3,2,1,0:T(8,128)}) custom-call(f32[2,16,24,128]{3,2,1,0:T(8,128)} %assemble.1.grid_ref), custom_call_target="tpu_custom_call" | custom-call | tf_op jit(solution)/shard_map/halo/pallas_call | solution.py:541
  62.3 13.2 %solve.1 = (f32[18,40,128]{2,1,0:T(8,128)}, f32[18,40,128]{2,1,0:T(8,128)}, f32[18,40,128]{2,1,0:T(8,128)}, f32[1,128]{1,0:T(1,128)}) custom-call(f32[2,16,24,128]{3,2,1,0:T(8,128)} %assemble.1.grid_ref, f32[2,2,6,24,128]{4,3,2,1,0:T(8,128)} %get-tuple-element.16.hx_ref, f32[2,2,16,8,128]{4,3,2,1,0:T(8,128)} %get-tuple-element.17.hy_ref, ...), custom_call_target="tpu_custom_call" | custom-call | tf_op jit(solution)/shard_map/solve/pallas_call | solution.py:550
  75.5 13.3 %lowest.1.lows_ref = f32[128,1,128]{2,1,0:T(1,128)} custom-call(f32[1,128]{1,0:T(1,128)} %get-tuple-element.22.low_ref), custom_call_target="tpu_custom_call" | custom-call | tf_op jit(solution)/shard_map/lowest/pallas_call | solution.py:561
  88.8 7.5 %pack.1.x_ref = f32[128,2,12,128]{3,2,1,0:T(8,128)} custom-call(f32[18,40,128]{2,1,0:T(8,128)} %get-tuple-element.19.a_ref, f32[18,40,128]{2,1,0:T(8,128)} %get-tuple-element.20.b_ref, f32[18,40,128]{2,1,0:T(8,128)} %get-tuple-element.21.c_ref, f32[128,1,128]{2,1,0:T(1,128)} %lowest.1.lows_ref, f32[1,768]{1,0:T(1,128)} %get-tuple-element.15.source_ref, ...), custom_call_target="tpu_custom_call" | custom-call | tf_op jit(solution)/shard_map/pack/pallas_call | solution.py:562
  96.3 29.4 %return.1.back_ref = f32[128,2,12,128]{3,2,1,0:T(8,128)} custom-call(f32[128,2,12,128]{3,2,1,0:T(8,128)} %pack.1.x_ref), custom_call_target="tpu_custom_call" | custom-call | tf_op jit(solution)/shard_map/return/pallas_call | solution.py:569
  125.7 15.2 %prolong.1 = f32[768,4096]{1,0:T(8,128)} custom-call(f32[128,2,12,128]{3,2,1,0:T(8,128)} %return.1.back_ref, f32[1,768]{1,0:T(1,128)} %get-tuple-element.14.target_ref, bf16[768,4096]{1,0:T(8,128)(2,1)} %t_ref.3, bf16[768,4096]{1,0:T(8,128)(2,1)} %k_ref.3, s32[1,768]{1,0:T(1,128)} %reshape.12.depth_ref, bf16[512,768]{1,0:T(8,128)(2,1)} %constant.10.clone.twice_ref, ...), custom_call_target="tpu_custom_call" | custom-call | tf_op jit(solution)/shard_map/prolong/pallas_call | solution.py:572
  (1 shorter events, 0.0 us)

commit v2 on v1

v2 whole, which is shorter than its diff:
```python
import jax
import jax.numpy as jnp
import numpy as np
from jax import lax
from jax.experimental import pallas as pl
from jax.experimental.pallas import tpu as pltpu
from jax.sharding import PartitionSpec as P

MESH = pl.DeviceIdType.MESH
F32 = jnp.float32
BF16 = jnp.bfloat16
BX, BY, BZ = 4, 6, 32
CX, CY = 16, 24
SLOTS = 768
NDEV = 128
CAP = 12
PAD = 16
ROWS = 128
XH, YH = 6, 8
EX, EY = CX + 2 * XH, CY + 2 * YH


def average_table():
    table = np.zeros((4, 2, 2, 8, 16, 4, 2, 4, 4), np.float32)
    for i in range(4):
        for bh in range(2):
            for f in range(2):
                for b in range(8):
                    for c in range(16):
                        table[i, bh, f, b, c, c // 4, f, i, 2 * bh + b // 4] = 1.0 / 64.0
    return jnp.asarray(table.reshape(8, 256, 128), BF16)


def select_table():
    table = np.zeros((BY, 6, 128, 128), np.float32)
    for v in range(BY):
        for l in range(6):
            for i in range(3):
                for j in range(6):
                    table[v, l, i * 40 + 7 + 4 * v + j, i * 42 + j * 6 + l] = 1.0
    return jnp.asarray(table.reshape(BY, 768, 128), BF16)


def twice_table():
    table = np.zeros((2, 2, 128, 6, 2, 64), np.float32)
    for i in range(6):
        for jl in range(36):
            table[:, i // 3, (i % 3) * 42 + jl, i, :, jl] = 1.0
    return jnp.asarray(table.reshape(512, 768), BF16)


def line_weights():
    weights = np.zeros((16, 6))
    for a in range(16):
        position = (a + 0.5) / 4 + 0.5
        low = int(np.floor(position))
        weights[a, low] += 1.0 - (position - low)
        weights[a, low + 1] += position - low
    return weights


def plane_table():
    w = line_weights()
    plane = np.zeros((2, 64, 256))
    plane[:, :36] = np.kron(w, w).T
    return jnp.asarray(plane.reshape(128, 256), BF16)


def halves(x):
    high = x.astype(BF16)
    return high, (x - high.astype(F32)).astype(BF16)


def dot(a, b):
    return jnp.dot(a, b, preferred_element_type=F32)


def column(row):
    return jnp.broadcast_to(row, (128, 128)).T


def lanes(shape):
    return lax.broadcasted_iota(jnp.int32, shape, len(shape) - 1)


def flipped(x, k):
    return (x, x + 1 - 2 * (x % 2), (x + 2) % 4, 3 - x)[k]


def hops(q):
    near = (0, 1, 2, 1)
    return near[q // 32] + near[q // 8 % 4] + near[q // 2 % 4]


def peer_ids():
    gx, gy = lax.axis_index("gx"), lax.axis_index("gy")
    xs = [flipped(gx // 4, k) * 4 for k in range(4)]
    ys = [flipped(gx % 4, k) for k in range(4)]
    zs = [flipped(gy // 2, k) * 2 for k in range(4)]
    cs = [gy % 2, 1 - gy % 2]
    return [(xs[q // 32] + ys[q // 8 % 4], zs[q // 2 % 4] + cs[q % 2]) for q in range(NDEV)]


CHUNKS = sorted(range(8), key=lambda c: -sum(hops(16 * c + t) for t in range(16)))


def chunk_peers(c):
    return sorted((q for q in range(16 * c, 16 * c + 16) if q), key=lambda q: -hops(q))


def remote(src, dst, send_sem, recv_sem, who):
    return pltpu.make_async_remote_copy(
        src_ref=src,
        dst_ref=dst,
        send_sem=send_sem,
        recv_sem=recv_sem,
        device_id=who,
        device_id_type=MESH,
    )


def rank_row(owner, key):
    owner_c = [column(owner[:, i * 128 : i * 128 + 128]) for i in range(6)]
    key_c = [column(key[:, i * 128 : i * 128 + 128]) for i in range(6)]
    out = []
    for j in range(6):
        ro, rk = owner[:, j * 128 : j * 128 + 128], key[:, j * 128 : j * 128 + 128]
        total = jnp.zeros((128, 128), F32)
        for i in range(6):
            total += jnp.where((owner_c[i] == ro) & (key_c[i] < rk), 1.0, 0.0)
        out.append(jnp.sum(total, axis=0, keepdims=True))
    return jnp.concatenate(out, axis=1)


def target_of(box):
    box = box.astype(F32)
    owner = jnp.floor((box + 0.5) * (1.0 / SLOTS))
    return owner * PAD + rank_row(owner, lanes((1, SLOTS)).astype(F32))


def source_of(slot):
    slot = slot.astype(F32)
    home = jnp.floor((slot + 0.5) * (1.0 / SLOTS))
    rows = home * PAD + rank_row(home, slot)
    group = lanes((1, 128)) // 32
    out = []
    for v in range(BY):
        mixed = None
        for u in range(BX):
            at = u * BY + v
            part = rows[:, at // 4 * 128 : at // 4 * 128 + 128]
            part = pltpu.roll(part, (u - at) * 32 % 128, 1)
            mixed = part if mixed is None else jnp.where(group == u, part, mixed)
        out.append(mixed)
    return jnp.concatenate(out, axis=1)


def one_hot(row, start, me):
    index = lax.broadcasted_iota(jnp.int32, (256, SLOTS), 0) + start
    index = jnp.bitwise_xor(index, jnp.broadcast_to(me * PAD, (256, SLOTS)))
    return jnp.where(index.astype(F32) == row, 1.0, 0.0).astype(BF16)


def restrict_block(step, t_ref, k_ref, depths, table_ref, glow_ref, held):
    at_row = pl.ds(pl.multiple_of(step * ROWS, ROWS), ROWS)
    depth = column(depths[pl.ds(step, 1), :])
    layer = (lanes((ROWS, 128)) % 16).astype(F32)
    mask = jnp.where(layer < depth, 4.0, 0.0)
    total = jnp.zeros((ROWS, 128), F32)
    for i in range(4):
        for bh in range(2):
            glow = absorb = None
            for a in range(4):
                at = (4 * i + a) * 256 + bh * 128
                t = t_ref[at_row, at : at + 128].astype(F32)
                k = k_ref[at_row, at : at + 128].astype(F32)
                square = t * t
                term = k * (square * square) * mask
                glow_ref[at_row, at : at + 128] = term
                glow = term if glow is None else glow + term
                absorb = k if absorb is None else absorb + k
            high, low = halves(jnp.concatenate([glow, absorb], axis=1))
            table = table_ref[2 * i + bh]
            total += dot(high, table) + dot(low, table)
    held[at_row, :] = total


def send_out(x_ref, make_block, put, o_ref, send_sem, recv_sems):
    ids = peer_ids()
    before = None
    for n, c in enumerate(CHUNKS + [None]):
        if c is not None:
            put(c, make_block(c))
        if before is not None:
            for q in chunk_peers(before):
                remote(x_ref.at[q], o_ref.at[q], send_sem, recv_sems.at[before], ids[q]).start()
        before = c
    o_ref[0] = x_ref[0]


def chunk_of(c):
    return pl.ds(1, 15) if c == 0 else pl.ds(16 * c, 16)


def padded_rows(value):
    n = value.shape[0]
    zeros = jnp.zeros((n, PAD - CAP, 128), F32)
    return jnp.concatenate([value, zeros], axis=1).reshape(n * PAD, 128)


def assemble(arrived, recv_sems, source, me, grid_ref):
    total = jnp.zeros((128, SLOTS), F32)
    for c in CHUNKS:
        pltpu.make_async_copy(
            arrived.at[chunk_of(c)], arrived.at[chunk_of(c)], recv_sems.at[c]
        ).wait()
        rows = padded_rows(arrived[16 * c : 16 * c + 16])
        high, low = halves(jnp.concatenate([rows[:128].T, rows[128:].T], axis=1))
        hot = one_hot(source, c * 256, me)
        total += dot(high, hot) + dot(low, hot)
    group = lanes((32, 128)) // 32
    for v in range(BY):
        for u in range(BX):
            out = None
            for l in range(4):
                part = total[l * 32 : l * 32 + 32, v * 128 : v * 128 + 128]
                part = pltpu.roll(part, (l - u) * 32 % 128, 1)
                out = part if out is None else jnp.where(group == l, part, out)
            for f in range(2):
                for i in range(4):
                    at = (f * 4 + i) * 4
                    grid_ref[f, 4 * u + i, 4 * v : 4 * v + 4, :] = out[at : at + 4]


def halo_copies(f, grid_ref, hx_ref, hy_ref, hc_ref, send_sem, recv_sem):
    gx, gy = lax.axis_index("gx"), lax.axis_index("gy")
    up_x, down_x = (gx + 1) % 16, (gx + 15) % 16
    up_y, down_y = (gy + 1) % 8, (gy + 7) % 8
    last_x, first_x = pl.ds(CX - XH, XH), pl.ds(0, XH)
    last_y, first_y = pl.ds(CY - YH, YH), pl.ds(0, YH)
    plan = [
        (grid_ref.at[f, last_x, last_y], hc_ref.at[f, 0], (up_x, up_y)),
        (grid_ref.at[f, last_x, first_y], hc_ref.at[f, 1], (up_x, down_y)),
        (grid_ref.at[f, first_x, last_y], hc_ref.at[f, 2], (down_x, up_y)),
        (grid_ref.at[f, first_x, first_y], hc_ref.at[f, 3], (down_x, down_y)),
        (grid_ref.at[f, last_x], hx_ref.at[f, 0], (up_x, gy)),
        (grid_ref.at[f, first_x], hx_ref.at[f, 1], (down_x, gy)),
        (grid_ref.at[f, :, last_y], hy_ref.at[f, 0], (gx, up_y)),
        (grid_ref.at[f, :, first_y], hy_ref.at[f, 1], (gx, down_y)),
    ]
    return [
        remote(src, dst, send_sem.at[f, n], recv_sem.at[f, n], who)
        for n, (src, dst, who) in enumerate(plan)
    ]


def spread_halo(f, ext, hx_ref, hy_ref, hc_ref):
    own_x, own_y = pl.ds(XH, CX), pl.ds(YH, CY)
    for side, at in ((0, 0), (1, XH + CX)):
        ext[f, pl.ds(at, XH), own_y] = hx_ref[f, side]
    for side, at in ((0, 0), (1, YH + CY)):
        ext[f, own_x, pl.ds(at, YH)] = hy_ref[f, side]
    for n, (atx, aty) in enumerate(
        ((0, 0), (0, YH + CY), (XH + CX, 0), (XH + CX, YH + CY))
    ):
        ext[f, pl.ds(atx, XH), pl.ds(aty, YH)] = hc_ref[f, n]


def z_lower(v):
    lane = lanes(v.shape)
    return jnp.where(lane < 32, pltpu.roll(v, 33, 1), pltpu.roll(v, 32, 1))


def z_upper(v):
    lane = lanes(v.shape)
    return jnp.where(lane >= 96, pltpu.roll(v, 95, 1), pltpu.roll(v, 96, 1))


def face(a, b):
    return (2.0 / 3.0) / (a + b)


def coefficients(ext, w):
    gx, gy = lax.axis_index("gx"), lax.axis_index("gy")
    shape = (EY, 128)
    row = lax.broadcasted_iota(jnp.int32, shape, 0)
    lane = lanes(shape)
    y_at = gy * CY + row - YH
    has_ym, has_yp = y_at >= 1, y_at <= 8 * CY - 2
    has_zm, has_zp = lane != 0, lane != 127

    def plane(x, low):
        x_at = gx * CX + x - XH
        k = ext[1, x]
        has_xm = jnp.broadcast_to(x_at, shape) >= 1
        has_xp = jnp.broadcast_to(x_at, shape) <= 16 * CX - 2
        near = (
            (has_xm, ext[1, x - 1]),
            (has_xp, ext[1, x + 1]),
            (has_ym, pltpu.roll(k, 1, 0)),
            (has_yp, pltpu.roll(k, EY - 1, 0)),
            (has_zm, z_lower(k)),
            (has_zp, z_upper(k)),
        )
        faces = [face(k, jnp.where(has, other, k)) for has, other in near]
        diagonal = k
        for c in faces:
            diagonal = diagonal + c
        inverse = 1.0 / diagonal
        for n, c in enumerate(faces):
            w[n, x] = jnp.where(near[n][0], c * inverse, 0.0)
        w[6, x] = inverse
        own = jnp.broadcast_to((x >= XH) & (x < XH + CX), shape)
        return jnp.minimum(low, jnp.where(own, k * inverse, 1.0))

    def pair(n, low):
        return plane(2 + 2 * n, plane(1 + 2 * n, low))

    low = lax.fori_loop(0, (EX - 2) // 2, pair, jnp.ones(shape, F32))
    low = jnp.min(low[YH : YH + CY], axis=0, keepdims=True)
    return jnp.min(low, axis=1, keepdims=True)


def powers(ext, w, v):
    for x in range(1, EX - 1):
        v[0, x] = w[6, x] * ext[0, x]
    for n, width in enumerate((4, 2, 4, 3)):
        count = (EX - 4 - 2 * n) // width

        def several(m, _, n=n, width=width):
            for t in range(width):
                x = 2 + n + m * width + t
                mid = v[n, x]
                v[n + 1, x] = (
                    w[0, x] * v[n, x - 1]
                    + w[1, x] * v[n, x + 1]
                    + w[2, x] * pltpu.roll(mid, 1, 0)
                    + w[3, x] * pltpu.roll(mid, EY - 1, 0)
                    + w[4, x] * z_lower(mid)
                    + w[5, x] * z_upper(mid)
                )
            return 0

        lax.fori_loop(0, count, several, 0)


def incident(v, lows, inc):
    gx, gy = lax.axis_index("gx"), lax.axis_index("gy")
    shape = (EY, 128)
    lowest = jnp.min(lows[...], axis=0)
    delta = 1.0 - jnp.broadcast_to(lowest, shape)
    square = delta * delta
    scale = 1.0 / (16.0 - 20.0 * square + 5.0 * square * square)
    outer = 16.0 * scale
    inner = outer - 20.0 * square * scale
    row = lax.broadcasted_iota(jnp.int32, shape, 0)
    first_row = (row == YH - 1) & jnp.broadcast_to(gy == 0, shape)
    last_row = (row == YH + CY) & jnp.broadcast_to(gy == 7, shape)
    for x in range(CX + 2):
        at = x + XH - 1
        value = v[0, at] + inner * (v[1, at] + v[2, at]) + outer * (v[3, at] + v[4, at])
        value = jnp.where(first_row, pltpu.roll(value, EY - 1, 0), value)
        inc[x] = jnp.where(last_row, pltpu.roll(value, 1, 0), value)
    inc[0] = jnp.where(jnp.broadcast_to(gx == 0, shape), inc[1], inc[0])
    inc[CX + 1] = jnp.where(jnp.broadcast_to(gx == 15, shape), inc[CX], inc[CX + 1])


def cut_windows(inc, table_ref, win):
    edge = lax.broadcasted_iota(jnp.int32, (32, 128), 0)
    for h in range(2):
        pieces = [[] for _ in range(6)]
        for u in range(BX):
            stack = [inc[4 * u + 3 * h + i] for i in range(3)]
            stack = jnp.concatenate([*stack, jnp.zeros((8, 128), F32)], axis=0).T
            part = [stack[l * 32 : l * 32 + 32] for l in range(4)]
            pieces[0].append(jnp.where(edge == 0, part[0], pltpu.roll(part[3], 1, 0)))
            for l in range(4):
                pieces[l + 1].append(part[l])
            pieces[5].append(jnp.where(edge == 31, part[3], pltpu.roll(part[0], 31, 0)))
        rows = jnp.concatenate([jnp.concatenate(p, axis=0) for p in pieces], axis=1)
        high, low = halves(rows)
        for v in range(BY):
            table = table_ref[v]
            top, rest = halves(dot(high, table) + dot(low, table))
            win[0, v * 128 : v * 128 + 128, h * 128 : h * 128 + 128] = top
            win[1, v * 128 : v * 128 + 128, h * 128 : h * 128 + 128] = rest


def couple_kernel(
    t_hbm, k_hbm, depth_hbm, boxes_hbm, places_hbm, average_hbm, select_hbm,
    back_ref, target_ref, glow_ref, k_ref,
    t_ref, depth_ref, boxes_ref, places_ref, average_ref, select_ref,
    depths, held, source_ref, outgoing, arrived, grid_ref, hx, hy, hc, ext, w, v,
    low_ref, lows, inc, win, leaving,
    t_sem, k_sem, small_sem,
    out_send, out_recv, halo_send, halo_recv, low_send, low_recv, back_send, back_recv,
):
    me = lax.axis_index("gx") * 8 + lax.axis_index("gy")
    barrier = pltpu.get_barrier_semaphore()
    steps = SLOTS // ROWS

    def block_copies(step):
        rows = pl.ds(pl.multiple_of(step * ROWS, ROWS), ROWS)
        return (
            pltpu.make_async_copy(t_hbm.at[rows], t_ref.at[rows], t_sem.at[step]),
            pltpu.make_async_copy(k_hbm.at[rows], k_ref.at[rows], k_sem.at[step]),
        )

    small = [
        pltpu.make_async_copy(src, dst, small_sem.at[n])
        for n, (src, dst) in enumerate(
            (
                (depth_hbm, depth_ref),
                (boxes_hbm, boxes_ref),
                (places_hbm, places_ref),
                (average_hbm, average_ref),
                (select_hbm, select_ref),
            )
        )
    ]
    for copy in small[:4]:
        copy.start()
    for step in range(steps):
        for copy in block_copies(step):
            copy.start()
    small[4].start()
    for who in peer_ids()[1:]:
        pl.semaphore_signal(barrier, inc=1, device_id=who, device_id_type=MESH)
    for copy in small[:4]:
        copy.wait()
    depth = depth_ref[...].astype(F32).reshape(1, SLOTS)
    for n in range(steps):
        depths[n : n + 1, :] = depth[:, n * ROWS : n * ROWS + ROWS]
    target_ref[...] = target_of(boxes_ref[...].reshape(1, SLOTS))
    source_ref[...] = source_of(places_ref[...].reshape(1, SLOTS))

    @pl.loop(0, steps)
    def _(step):
        for copy in block_copies(step):
            copy.wait()
        restrict_block(step, t_ref, k_ref, depths, average_ref, glow_ref, held)

    small[4].wait()
    high, low = halves(held[...])
    target, source = target_ref[...], source_ref[...]
    pl.semaphore_wait(barrier, NDEV - 1)

    def to_owner(c):
        hot = one_hot(target, c * 256, me)
        return dot(hot, high) + dot(hot, low)

    def put_out(c, block):
        outgoing[16 * c : 16 * c + 16] = block.reshape(16, PAD, 128)[:, :CAP]

    send_out(outgoing, to_owner, put_out, arrived, out_send, out_recv)
    assemble(arrived, out_recv, source, me, grid_ref)
    ext[1, pl.ds(XH, CX), pl.ds(YH, CY)] = grid_ref[1]
    copies = [
        halo_copies(f, grid_ref, hx, hy, hc, halo_send, halo_recv) for f in range(2)
    ]
    for f in (1, 0):
        for copy in copies[f]:
            copy.start()
    ext[0, pl.ds(XH, CX), pl.ds(YH, CY)] = grid_ref[0]
    for copy in copies[1]:
        copy.wait()
    spread_halo(1, ext, hx, hy, hc)
    low_ref[...] = jnp.broadcast_to(coefficients(ext, w), (1, 128))
    for copy in copies[0]:
        copy.wait()
    spread_halo(0, ext, hx, hy, hc)
    ids = peer_ids()
    for q in sorted(range(1, NDEV), key=lambda q: -hops(q)):
        remote(low_ref, lows.at[q], low_send, low_recv, ids[q]).start()
    lows[0] = low_ref[...]
    powers(ext, w, v)
    others = pl.ds(1, NDEV - 1)
    pltpu.make_async_copy(lows.at[others], lows.at[others], low_recv).wait()
    incident(v, lows, inc)
    cut_windows(inc, select_ref, win)

    def to_slots(c):
        hot = one_hot(source, c * 256, me)
        return dot(hot, win[0]) + dot(hot, win[1])

    def put_back(c, block):
        for h in range(2):
            part = block[:, h * 128 : h * 128 + 128].reshape(16, PAD, 128)
            leaving[16 * c : 16 * c + 16, h] = part[:, :CAP]

    send_out(leaving, to_slots, put_back, back_ref, back_send, back_recv)
    for c in CHUNKS:
        pltpu.make_async_copy(
            back_ref.at[chunk_of(c)], back_ref.at[chunk_of(c)], back_recv.at[c]
        ).wait()
    pltpu.make_async_copy(lows.at[others], lows.at[others], low_send).wait()
    pltpu.make_async_copy(outgoing.at[others], outgoing.at[others], out_send).wait()
    pltpu.make_async_copy(leaving.at[others], leaving.at[others], back_send).wait()


def prolong_kernel(back_ref, target_ref, k_ref, glow_ref, twice_ref, plane_ref, out_ref, held):
    step = pl.program_id(0)
    me = lax.axis_index("gx") * 8 + lax.axis_index("gy")

    @pl.when(step == 0)
    def _():
        for h in range(2):
            high, low = halves(padded_rows(back_ref[:, h]))
            held[:, h * 128 : h * 128 + 128] = high
            held[:, 256 + h * 128 : 256 + h * 128 + 128] = low

    at_row = pl.ds(pl.multiple_of(step * ROWS, ROWS), ROWS)
    target = column(target_ref[:, at_row])
    place = jnp.bitwise_xor(lanes((ROWS, NDEV * PAD)), jnp.broadcast_to(me * PAD, (ROWS, NDEV * PAD)))
    place = place.astype(F32)
    hot = jnp.concatenate(
        [
            jnp.where(place[:, c * 128 : c * 128 + 128] == target, 1.0, 0.0).astype(BF16)
            for c in range(PAD)
        ],
        axis=1,
    )
    mine = dot(hot, held[...]).astype(BF16)
    both = dot(mine, twice_ref[...])
    first = lanes((ROWS, 128)) < 64
    weights = line_weights()
    plane = plane_ref[...]
    for a in range(16):
        low = int(np.flatnonzero(weights[a])[0])
        value = float(weights[a, low]) * both[:, low * 128 : low * 128 + 128] + float(
            weights[a, low + 1]
        ) * both[:, low * 128 + 128 : low * 128 + 256]
        rest = value - value.astype(BF16).astype(F32)
        fine = dot(jnp.where(first, value, rest).astype(BF16), plane)
        at = slice(a * 256, a * 256 + 256)
        out_ref[:, at] = k_ref[at_row, at].astype(F32) * fine - glow_ref[at_row, at]


VM = pl.BlockSpec(memory_space=pltpu.VMEM)
HB = pl.BlockSpec(memory_space=pltpu.HBM)
MIB = 1024 * 1024


def struct(*shape):
    return jax.ShapeDtypeStruct(shape, F32)


def on_device(thermal_state, opacity_field, glowing_depth, position_to_tile, tile_to_position):
    dma = pltpu.SemaphoreType.DMA
    steps = SLOTS // ROWS
    wide = pl.BlockSpec((ROWS, 4096), lambda i: (i, 0))

    def vmem(*shape, dtype=F32):
        return pltpu.VMEM(shape, dtype)

    back, target, glow, absorb = pl.pallas_call(
        couple_kernel,
        out_shape=[
            vmem(NDEV, 2, CAP, 128),
            vmem(1, SLOTS),
            vmem(SLOTS, 4096),
            vmem(SLOTS, 4096, dtype=BF16),
        ],
        in_specs=[HB] * 7,
        out_specs=[VM] * 4,
        scratch_shapes=[
            vmem(SLOTS, 4096, dtype=BF16),
            vmem(SLOTS, dtype=jnp.int32),
            vmem(SLOTS, dtype=jnp.int32),
            vmem(SLOTS, dtype=jnp.int32),
            vmem(8, 256, 128, dtype=BF16),
            vmem(BY, 768, 128, dtype=BF16),
            vmem(8, 128),
            vmem(SLOTS, 128),
            vmem(1, SLOTS),
            vmem(NDEV, CAP, 128),
            vmem(NDEV, CAP, 128),
            vmem(2, CX, CY, 128),
            vmem(2, 2, XH, CY, 128),
            vmem(2, 2, CX, YH, 128),
            vmem(2, 4, XH, YH, 128),
            vmem(2, EX, EY, 128),
            vmem(7, EX, EY, 128),
            vmem(5, EX, EY, 128),
            vmem(1, 128),
            vmem(NDEV, 1, 128),
            vmem(CX + 2, EY, 128),
            vmem(2, SLOTS, 256, dtype=BF16),
            vmem(NDEV, 2, CAP, 128),
            dma((steps,)),
            dma((steps,)),
            dma((5,)),
            dma,
            dma((8,)),
            dma((2, 8)),
            dma((2, 8)),
            dma,
            dma,
            dma,
            dma((8,)),
        ],
        compiler_params=pltpu.CompilerParams(
            collective_id=0, has_side_effects=True, vmem_limit_bytes=30 * MIB
        ),
        name="couple",
    )(
        *(
            pltpu.with_memory_space_constraint(x, pltpu.HBM)
            for x in (
                thermal_state,
                opacity_field,
                glowing_depth,
                position_to_tile,
                tile_to_position,
                average_table(),
                select_table(),
            )
        )
    )
    return pl.pallas_call(
        prolong_kernel,
        out_shape=struct(SLOTS, 4096),
        grid=(steps,),
        in_specs=[VM, VM, VM, VM, VM, VM],
        out_specs=wide,
        scratch_shapes=[pltpu.VMEM((NDEV * PAD, 512), BF16)],
        compiler_params=pltpu.CompilerParams(vmem_limit_bytes=20 * MIB),
        name="prolong",
    )(
        *(pltpu.with_memory_space_constraint(x, pltpu.VMEM) for x in (back, target, absorb, glow)),
        twice_table(),
        plane_table(),
    )


def solution(mesh):
    rows = P(("gx", "gy"), None)
    ints = P(("gx", "gy"))
    return jax.shard_map(
        on_device,
        mesh=mesh,
        in_specs=(rows, rows, ints, ints, ints),
        out_specs=rows,
        check_vma=False,
    )
```

time: 142 us -> 82.2 us (0.58)
  Pallas kernels: 137 us -> 82.1 us
  local copies, waits for them, and re-layouts: 3.98 us -> 0.01 us
    pallas_call x9 -> x1, Pallas kernels: 122 us -> 72.7 us  [on_device(): pl.pallas_call(couple_kernel, out_shape=[vmem(NDEV, 2, CAP, 128), vmem(1,...]
    pallas_call x1, Pallas kernels: 15.2 us -> 9.4 us  [on_device(): pl.pallas_call(prolong_kernel, out_shape=struct(SLOTS, 4096), grid=(steps...]
    reshape x4 -> x0, local copies, waits for them, and re-layouts: 3.97 us -> none  [the longest x2 1.43 us: on_device(): tile_to_position.reshape(BX, BY, BZ).transpose(1, 0, 2).reshape(1, SLOTS)]
where the time goes in v2:
time: 82.2 us; the launch traced here: 82.1 us
  Pallas kernels  82.1 us (100%)
    pallas_call x1, Pallas kernels, on_device(): pl.pallas_call(couple_kernel, out_shape=[vmem(NDEV, 2, CAP, 128), vmem(1,...  72.7 us
    pallas_call x1, Pallas kernels, on_device(): pl.pallas_call(prolong_kernel, out_shape=struct(SLOTS, 4096), grid=(steps...  9.4 us

profile of v2, /device:TPU:1, one launch (start us, length us, event | category | flops | bytes accessed | tf_op | source)
XLA Modules:
  0.0 82.1 jit_solution(1327515996856212477)
XLA Ops:
  0.0 0.0 copy-start
  0.0 0.0 copy-start.1
  0.0 72.7 %couple.1 = (f32[128,2,12,128]{3,2,1,0:T(8,128)S(1)}, f32[1,768]{1,0:T(1,128)S(1)}, f32[768,4096]{1,0:T(8,128)S(1)}, bf16[768,4096]{1,0:T(8,128)(2,1)S(1)}) custom-call(bf16[768,4096]{1,0:T(8,128)(2,1)} %t_hbm.1, bf16[768,4096]{1,0:T(8,128)(2,1)} %k_hbm.1, s32[768]{0:T(1024)} %depth_hbm.1, s32[768]{0:T(1024)} %boxes_hbm.1, s32[768]{0:T(1024)} %places_hbm.1, ...), custom_call_target="tpu_custom_call" | custom-call | tf_op jit(solution)/shard_map/couple/pallas_call | solution.py:556
  72.7 0.0 copy-done
  72.7 0.0 copy-done.1
  72.7 9.4 %prolong.1 = f32[768,4096]{1,0:T(8,128)} custom-call(f32[128,2,12,128]{3,2,1,0:T(8,128)S(1)} %get-tuple-element.9.back_ref, f32[1,768]{1,0:T(1,128)S(1)} %get-tuple-element.10.target_ref, bf16[768,4096]{1,0:T(8,128)(2,1)S(1)} %get-tuple-element.11.k_ref, f32[768,4096]{1,0:T(8,128)S(1)} %get-tuple-element.12.glow_ref, bf16[512,768]{1,0:T(8,128)(2,1)S(1)} %copy-done, ...), custom_call_target="tpu_custom_call" | custom-call | tf_op jit(solution)/shard_map/prolong/pallas_call | solution.py:620
Async XLA Ops:
  0.0 72.7 %copy-start = (bf16[512,768]{1,0:T(8,128)(2,1)S(1)}, bf16[512,768]{1,0:T(8,128)(2,1)}, u32[]{:S(2)}) copy-start(bf16[512,768]{1,0:T(8,128)(2,1)} %constant.10.clone.twice_ref) | copy-start | bytes 2359300
  0.0 72.7 %copy-start.1 = (bf16[128,256]{1,0:T(8,128)(2,1)S(1)}, bf16[128,256]{1,0:T(8,128)(2,1)}, u32[]{:S(2)}) copy-start(bf16[128,256]{1,0:T(8,128)(2,1)} %constant.11.clone.plane_ref) | copy-start | bytes 196612

commit v3 on v2

--- a/solution.py
+++ b/solution.py
@@ -32,13 +32,12 @@
 
 
 def select_table():
-    table = np.zeros((BY, 6, 128, 128), np.float32)
-    for v in range(BY):
-        for l in range(6):
-            for i in range(3):
-                for j in range(6):
-                    table[v, l, i * 40 + 7 + 4 * v + j, i * 42 + j * 6 + l] = 1.0
-    return jnp.asarray(table.reshape(BY, 768, 128), BF16)
+    table = np.zeros((6, 128, 128), np.float32)
+    for l in range(6):
+        for i in range(3):
+            for j in range(6):
+                table[l, i * 40 + 7 + j, i * 42 + j * 6 + l] = 1.0
+    return jnp.asarray(table, BF16)
 
 
 def twice_table():
@@ -101,11 +100,25 @@
     return [(xs[q // 32] + ys[q // 8 % 4], zs[q // 2 % 4] + cs[q % 2]) for q in range(NDEV)]
 
 
-CHUNKS = sorted(range(8), key=lambda c: -sum(hops(16 * c + t) for t in range(16)))
-
-
-def chunk_peers(c):
-    return sorted((q for q in range(16 * c, 16 * c + 16) if q), key=lambda q: -hops(q))
+CHUNKS = range(8)
+
+
+def peer_of(block):
+    t = block % 16
+    return t * 8 + (block // 16 ^ t % 8)
+
+
+def chunk_blocks(c):
+    return sorted(
+        (n for n in range(16 * c, 16 * c + 16) if n), key=lambda n: -hops(peer_of(n))
+    )
+
+
+def place_index(shape, dim, me, start=0):
+    row = lax.broadcasted_iota(jnp.int32, shape, dim) + start
+    t = row // PAD % 16
+    peer = jnp.bitwise_xor(t * 8 + jnp.bitwise_xor(t % 8, row // 256), jnp.broadcast_to(me, shape))
+    return peer * PAD + row % PAD
 
 
 def remote(src, dst, send_sem, recv_sem, who):
@@ -155,10 +168,15 @@
     return jnp.concatenate(out, axis=1)
 
 
-def one_hot(row, start, me):
-    index = lax.broadcasted_iota(jnp.int32, (256, SLOTS), 0) + start
-    index = jnp.bitwise_xor(index, jnp.broadcast_to(me * PAD, (256, SLOTS)))
-    return jnp.where(index.astype(F32) == row, 1.0, 0.0).astype(BF16)
+def one_hot(row, base, c):
+    index = jnp.bitwise_xor(base, c * PAD).astype(F32)
+    return jnp.concatenate(
+        [
+            jnp.where(index == row[:, n * 128 : n * 128 + 128], 1.0, 0.0).astype(BF16)
+            for n in range(SLOTS // 128)
+        ],
+        axis=1,
+    )
 
 
 def restrict_block(step, t_ref, k_ref, depths, table_ref, glow_ref, held):
@@ -188,18 +206,21 @@
 def send_out(x_ref, make_block, put, o_ref, send_sem, recv_sems):
     ids = peer_ids()
     before = None
-    for n, c in enumerate(CHUNKS + [None]):
+    for c in (*CHUNKS, None):
         if c is not None:
             put(c, make_block(c))
         if before is not None:
-            for q in chunk_peers(before):
-                remote(x_ref.at[q], o_ref.at[q], send_sem, recv_sems.at[before], ids[q]).start()
+            for n in chunk_blocks(before):
+                remote(
+                    x_ref.at[n], o_ref.at[n], send_sem, recv_sems.at[before], ids[peer_of(n)]
+                ).start()
         before = c
     o_ref[0] = x_ref[0]
 
 
-def chunk_of(c):
-    return pl.ds(1, 15) if c == 0 else pl.ds(16 * c, 16)
+def wait_chunk(o_ref, recv_sems, c):
+    blocks = pl.ds(1, 15) if c == 0 else pl.ds(16 * c, 16)
+    pltpu.make_async_copy(o_ref.at[blocks], o_ref.at[blocks], recv_sems.at[c]).wait()
 
 
 def padded_rows(value):
@@ -208,15 +229,13 @@
     return jnp.concatenate([value, zeros], axis=1).reshape(n * PAD, 128)
 
 
-def assemble(arrived, recv_sems, source, me, grid_ref):
+def assemble(arrived, recv_sems, source, base, grid_ref):
     total = jnp.zeros((128, SLOTS), F32)
     for c in CHUNKS:
-        pltpu.make_async_copy(
-            arrived.at[chunk_of(c)], arrived.at[chunk_of(c)], recv_sems.at[c]
-        ).wait()
+        wait_chunk(arrived, recv_sems, c)
         rows = padded_rows(arrived[16 * c : 16 * c + 16])
         high, low = halves(jnp.concatenate([rows[:128].T, rows[128:].T], axis=1))
-        hot = one_hot(source, c * 256, me)
+        hot = one_hot(source, base, c)
         total += dot(high, hot) + dot(low, hot)
     group = lanes((32, 128)) // 32
     for v in range(BY):
@@ -388,9 +407,9 @@
 
 def couple_kernel(
     t_hbm, k_hbm, depth_hbm, boxes_hbm, places_hbm, average_hbm, select_hbm,
-    back_ref, target_ref, glow_ref, k_ref,
-    t_ref, depth_ref, boxes_ref, places_ref, average_ref, select_ref,
-    depths, held, source_ref, outgoing, arrived, grid_ref, hx, hy, hc, ext, w, v,
+    mine_ref, glow_ref, k_ref,
+    t_ref, depth_ref, boxes_ref, places_ref, average_ref, first_ref, select_ref,
+    back_ref, target_ref, target_c, depths, held, source_ref, outgoing, arrived, grid_ref, hx, hy, hc, ext, w, v,
     low_ref, lows, inc, win, leaving,
     t_sem, k_sem, small_sem,
     out_send, out_recv, halo_send, halo_recv, low_send, low_recv, back_send, back_recv,
@@ -414,65 +433,84 @@
                 (boxes_hbm, boxes_ref),
                 (places_hbm, places_ref),
                 (average_hbm, average_ref),
-                (select_hbm, select_ref),
+                (select_hbm, first_ref),
             )
         )
     ]
-    for copy in small[:4]:
+    for copy in small[:3]:
         copy.start()
-    for step in range(steps):
-        for copy in block_copies(step):
-            copy.start()
-    small[4].start()
+    for copy in (*block_copies(0), small[3], *block_copies(1)):
+        copy.start()
     for who in peer_ids()[1:]:
         pl.semaphore_signal(barrier, inc=1, device_id=who, device_id_type=MESH)
-    for copy in small[:4]:
+    for copy in small[:3]:
         copy.wait()
     depth = depth_ref[...].astype(F32).reshape(1, SLOTS)
     for n in range(steps):
         depths[n : n + 1, :] = depth[:, n * ROWS : n * ROWS + ROWS]
     target_ref[...] = target_of(boxes_ref[...].reshape(1, SLOTS))
-    source_ref[...] = source_of(places_ref[...].reshape(1, SLOTS))
+    small[3].wait()
 
     @pl.loop(0, steps)
     def _(step):
+        @pl.when(step + 2 < steps)
+        def _():
+            for copy in block_copies(step + 2):
+                copy.start()
+
         for copy in block_copies(step):
             copy.wait()
         restrict_block(step, t_ref, k_ref, depths, average_ref, glow_ref, held)
 
-    small[4].wait()
     high, low = halves(held[...])
-    target, source = target_ref[...], source_ref[...]
+    target = target_ref[...]
+    base = place_index((256, 128), 0, me)
     pl.semaphore_wait(barrier, NDEV - 1)
 
     def to_owner(c):
-        hot = one_hot(target, c * 256, me)
+        hot = one_hot(target, base, c)
         return dot(hot, high) + dot(hot, low)
 
     def put_out(c, block):
         outgoing[16 * c : 16 * c + 16] = block.reshape(16, PAD, 128)[:, :CAP]
 
     send_out(outgoing, to_owner, put_out, arrived, out_send, out_recv)
-    assemble(arrived, out_recv, source, me, grid_ref)
+    small[4].start()
+    source_ref[...] = source_of(places_ref[...].reshape(1, SLOTS))
+    for n in range(steps):
+        target_c[n * ROWS : n * ROWS + ROWS, :] = column(target[:, n * ROWS : n * ROWS + ROWS])
+    source = source_ref[...]
+    small[4].wait()
+    for l in range(6):
+        table = first_ref[l].astype(F32)
+        for v_at in range(BY):
+            moved = pltpu.roll(table, 4 * v_at, 0) if v_at else table
+            select_ref[v_at, l * 128 : l * 128 + 128] = moved.astype(BF16)
+    assemble(arrived, out_recv, source, base, grid_ref)
     ext[1, pl.ds(XH, CX), pl.ds(YH, CY)] = grid_ref[1]
     copies = [
         halo_copies(f, grid_ref, hx, hy, hc, halo_send, halo_recv) for f in range(2)
     ]
-    for f in (1, 0):
-        for copy in copies[f]:
-            copy.start()
+    for copy in copies[1]:
+        copy.start()
     ext[0, pl.ds(XH, CX), pl.ds(YH, CY)] = grid_ref[0]
     for copy in copies[1]:
-        copy.wait()
+        copy.wait_send()
+    for copy in copies[0]:
+        copy.start()
+    for copy in copies[1]:
+        copy.wait_recv()
     spread_halo(1, ext, hx, hy, hc)
     low_ref[...] = jnp.broadcast_to(coefficients(ext, w), (1, 128))
-    for copy in copies[0]:
+    for copy in copies[0][6:]:
         copy.wait()
-    spread_halo(0, ext, hx, hy, hc)
     ids = peer_ids()
     for q in sorted(range(1, NDEV), key=lambda q: -hops(q)):
         remote(low_ref, lows.at[q], low_send, low_recv, ids[q]).start()
     lows[0] = low_ref[...]
+    for copy in copies[0][:6]:
+        copy.wait()
+    spread_halo(0, ext, hx, hy, hc)
     powers(ext, w, v)
     others = pl.ds(1, NDEV - 1)
     pltpu.make_async_copy(lows.at[others], lows.at[others], low_recv).wait()
@@ -480,7 +518,7 @@
     cut_windows(inc, select_ref, win)
 
     def to_slots(c):
-        hot = one_hot(source, c * 256, me)
+        hot = one_hot(source, base, c)
         return dot(hot, win[0]) + dot(hot, win[1])
 
     def put_back(c, block):
@@ -489,39 +527,36 @@
             leaving[16 * c : 16 * c + 16, h] = part[:, :CAP]
 
     send_out(leaving, to_slots, put_back, back_ref, back_send, back_recv)
+    across = place_index((1, 256), 1, me)
     for c in CHUNKS:
-        pltpu.make_async_copy(
-            back_ref.at[chunk_of(c)], back_ref.at[chunk_of(c)], back_recv.at[c]
-        ).wait()
+        wait_chunk(back_ref, back_recv, c)
+        parts = [
+            halves(padded_rows(back_ref[16 * c : 16 * c + 16, h])) for h in range(2)
+        ]
+        rows = jnp.concatenate([part[k] for k in range(2) for part in parts], axis=1)
+        index = jnp.bitwise_xor(across, c * PAD).astype(F32)
+        for n in range(steps):
+            at = slice(n * ROWS, n * ROWS + ROWS)
+            hot = jnp.concatenate(
+                [
+                    jnp.where(
+                        index[:, m * 128 : m * 128 + 128] == target_c[at, :], 1.0, 0.0
+                    ).astype(BF16)
+                    for m in range(2)
+                ],
+                axis=1,
+            )
+            found = dot(hot, rows).astype(BF16)
+            mine_ref[at, :] = found if c == 0 else mine_ref[at, :] + found
     pltpu.make_async_copy(lows.at[others], lows.at[others], low_send).wait()
     pltpu.make_async_copy(outgoing.at[others], outgoing.at[others], out_send).wait()
     pltpu.make_async_copy(leaving.at[others], leaving.at[others], back_send).wait()
 
 
-def prolong_kernel(back_ref, target_ref, k_ref, glow_ref, twice_ref, plane_ref, out_ref, held):
+def prolong_kernel(mine_ref, k_ref, glow_ref, twice_ref, plane_ref, out_ref):
     step = pl.program_id(0)
-    me = lax.axis_index("gx") * 8 + lax.axis_index("gy")
-
-    @pl.when(step == 0)
-    def _():
-        for h in range(2):
-            high, low = halves(padded_rows(back_ref[:, h]))
-            held[:, h * 128 : h * 128 + 128] = high
-            held[:, 256 + h * 128 : 256 + h * 128 + 128] = low
-
     at_row = pl.ds(pl.multiple_of(step * ROWS, ROWS), ROWS)
-    target = column(target_ref[:, at_row])
-    place = jnp.bitwise_xor(lanes((ROWS, NDEV * PAD)), jnp.broadcast_to(me * PAD, (ROWS, NDEV * PAD)))
-    place = place.astype(F32)
-    hot = jnp.concatenate(
-        [
-            jnp.where(place[:, c * 128 : c * 128 + 128] == target, 1.0, 0.0).astype(BF16)
-            for c in range(PAD)
-        ],
-        axis=1,
-    )
-    mine = dot(hot, held[...]).astype(BF16)
-    both = dot(mine, twice_ref[...])
+    both = dot(mine_ref[at_row, :], twice_ref[...])
     first = lanes((ROWS, 128)) < 64
     weights = line_weights()
     plane = plane_ref[...]
@@ -553,23 +588,26 @@
     def vmem(*shape, dtype=F32):
         return pltpu.VMEM(shape, dtype)
 
-    back, target, glow, absorb = pl.pallas_call(
+    mine, glow, absorb = pl.pallas_call(
         couple_kernel,
         out_shape=[
-            vmem(NDEV, 2, CAP, 128),
-            vmem(1, SLOTS),
+            vmem(SLOTS, 512, dtype=BF16),
             vmem(SLOTS, 4096),
             vmem(SLOTS, 4096, dtype=BF16),
         ],
         in_specs=[HB] * 7,
-        out_specs=[VM] * 4,
+        out_specs=[VM] * 3,
         scratch_shapes=[
             vmem(SLOTS, 4096, dtype=BF16),
             vmem(SLOTS, dtype=jnp.int32),
             vmem(SLOTS, dtype=jnp.int32),
             vmem(SLOTS, dtype=jnp.int32),
             vmem(8, 256, 128, dtype=BF16),
+            vmem(6, 128, 128, dtype=BF16),
             vmem(BY, 768, 128, dtype=BF16),
+            vmem(NDEV, 2, CAP, 128),
+            vmem(1, SLOTS),
+            vmem(SLOTS, 128),
             vmem(8, 128),
             vmem(SLOTS, 128),
             vmem(1, SLOTS),
@@ -621,13 +659,12 @@
         prolong_kernel,
         out_shape=struct(SLOTS, 4096),
         grid=(steps,),
-        in_specs=[VM, VM, VM, VM, VM, VM],
+        in_specs=[VM] * 5,
         out_specs=wide,
-        scratch_shapes=[pltpu.VMEM((NDEV * PAD, 512), BF16)],
         compiler_params=pltpu.CompilerParams(vmem_limit_bytes=20 * MIB),
         name="prolong",
     )(
-        *(pltpu.with_memory_space_constraint(x, pltpu.VMEM) for x in (back, target, absorb, glow)),
+        *(pltpu.with_memory_space_constraint(x, pltpu.VMEM) for x in (mine, absorb, glow)),
         twice_table(),
         plane_table(),
     )

time: 82.2 us -> 71.3 us (0.87)
  Pallas kernels: 82.1 us -> 71.1 us
    pallas_call x1, Pallas kernels: 72.7 us -> 64.1 us  [on_device(): pl.pallas_call(couple_kernel, out_shape=[vmem(SLOTS, 512, dtype=BF16), vm...]
    pallas_call x1, Pallas kernels: 9.4 us -> 7.06 us  [on_device(): pl.pallas_call(prolong_kernel, out_shape=struct(SLOTS, 4096), grid=(steps...]
where the time goes in v3:
time: 71.3 us; the launch traced here: 71.1 us
  Pallas kernels  71.1 us (100%)
    pallas_call x1, Pallas kernels, on_device(): pl.pallas_call(couple_kernel, out_shape=[vmem(SLOTS, 512, dtype=BF16), vm...  64.1 us
    pallas_call x1, Pallas kernels, on_device(): pl.pallas_call(prolong_kernel, out_shape=struct(SLOTS, 4096), grid=(steps...  7.06 us

profile of v3, /device:TPU:1, one launch (start us, length us, event | category | flops | bytes accessed | tf_op | source)
XLA Modules:
  0.0 71.1 jit_solution(2067758454236618958)
XLA Ops:
  0.0 0.0 copy-start
  0.0 0.0 copy-start.1
  0.0 64.1 %couple.1 = (bf16[768,512]{1,0:T(8,128)(2,1)S(1)}, f32[768,4096]{1,0:T(8,128)S(1)}, bf16[768,4096]{1,0:T(8,128)(2,1)S(1)}) custom-call(bf16[768,4096]{1,0:T(8,128)(2,1)} %t_hbm.1, bf16[768,4096]{1,0:T(8,128)(2,1)} %k_hbm.1, s32[768]{0:T(1024)} %depth_hbm.1, s32[768]{0:T(1024)} %boxes_hbm.1, s32[768]{0:T(1024)} %places_hbm.1, ...), custom_call_target="tpu_custom_call" | custom-call | tf_op jit(solution)/shard_map/couple/pallas_call | solution.py:591
  64.1 0.0 copy-done
  64.1 0.0 copy-done.1
  64.1 7.1 %prolong.1 = f32[768,4096]{1,0:T(8,128)} custom-call(bf16[768,512]{1,0:T(8,128)(2,1)S(1)} %get-tuple-element.8.mine_ref, bf16[768,4096]{1,0:T(8,128)(2,1)S(1)} %get-tuple-element.9.k_ref, f32[768,4096]{1,0:T(8,128)S(1)} %get-tuple-element.10.glow_ref, bf16[512,768]{1,0:T(8,128)(2,1)S(1)} %copy-done, bf16[128,256]{1,0:T(8,128)(2,1)S(1)} %copy-done.1), custom_call_target="tpu_custom_call" | custom-call | tf_op jit(solution)/shard_map/prolong/pallas_call | solution.py:658
Async XLA Ops:
  0.0 64.1 %copy-start = (bf16[512,768]{1,0:T(8,128)(2,1)S(1)}, bf16[512,768]{1,0:T(8,128)(2,1)}, u32[]{:S(2)}) copy-start(bf16[512,768]{1,0:T(8,128)(2,1)} %constant.10.clone.twice_ref) | copy-start | bytes 2359300
  0.0 64.1 %copy-start.1 = (bf16[128,256]{1,0:T(8,128)(2,1)S(1)}, bf16[128,256]{1,0:T(8,128)(2,1)}, u32[]{:S(2)}) copy-start(bf16[128,256]{1,0:T(8,128)(2,1)} %constant.11.clone.plane_ref) | copy-start | bytes 196612

commit v4 on v3

--- a/solution.py
+++ b/solution.py
@@ -15,6 +15,7 @@
 NDEV = 128
 CAP = 12
 PAD = 16
+LINES = 21
 ROWS = 128
 XH, YH = 6, 8
 EX, EY = CX + 2 * XH, CY + 2 * YH
@@ -31,20 +32,18 @@
     return jnp.asarray(table.reshape(8, 256, 128), BF16)
 
 
-def select_table():
-    table = np.zeros((6, 128, 128), np.float32)
-    for l in range(6):
-        for i in range(3):
-            for j in range(6):
-                table[l, i * 40 + 7 + j, i * 42 + j * 6 + l] = 1.0
-    return jnp.asarray(table, BF16)
+def select_keys():
+    keys = np.full((8, 256), -100000, np.int32)
+    for n in range(216):
+        i, j, l = n // 36, n % 36 // 6, n % 6
+        keys[i // 3, n] = l * 128 + i % 3 * 40 + 7 + j
+    return jnp.asarray(keys)
 
 
 def twice_table():
-    table = np.zeros((2, 2, 128, 6, 2, 64), np.float32)
-    for i in range(6):
-        for jl in range(36):
-            table[:, i // 3, (i % 3) * 42 + jl, i, :, jl] = 1.0
+    table = np.zeros((2, 256, 6, 2, 64), np.float32)
+    for n in range(216):
+        table[:, n, n // 36, :, n % 36] = 1.0
     return jnp.asarray(table.reshape(512, 768), BF16)
 
 
@@ -190,7 +189,7 @@
             glow = absorb = None
             for a in range(4):
                 at = (4 * i + a) * 256 + bh * 128
-                t = t_ref[at_row, at : at + 128].astype(F32)
+                t = t_ref[step % 3, :, at : at + 128].astype(F32)
                 k = k_ref[at_row, at : at + 128].astype(F32)
                 square = t * t
                 term = k * (square * square) * mask
@@ -255,34 +254,57 @@
     gx, gy = lax.axis_index("gx"), lax.axis_index("gy")
     up_x, down_x = (gx + 1) % 16, (gx + 15) % 16
     up_y, down_y = (gy + 1) % 8, (gy + 7) % 8
-    last_x, first_x = pl.ds(CX - XH, XH), pl.ds(0, XH)
     last_y, first_y = pl.ds(CY - YH, YH), pl.ds(0, YH)
+    deep = XH if f else XH - 1
+    low, high = pl.ds(XH - deep, deep), pl.ds(0, deep)
+    sent_low, sent_high = pl.ds(CX - deep, deep), pl.ds(0, deep)
     plan = [
-        (grid_ref.at[f, last_x, last_y], hc_ref.at[f, 0], (up_x, up_y)),
-        (grid_ref.at[f, last_x, first_y], hc_ref.at[f, 1], (up_x, down_y)),
-        (grid_ref.at[f, first_x, last_y], hc_ref.at[f, 2], (down_x, up_y)),
-        (grid_ref.at[f, first_x, first_y], hc_ref.at[f, 3], (down_x, down_y)),
-        (grid_ref.at[f, last_x], hx_ref.at[f, 0], (up_x, gy)),
-        (grid_ref.at[f, first_x], hx_ref.at[f, 1], (down_x, gy)),
         (grid_ref.at[f, :, last_y], hy_ref.at[f, 0], (gx, up_y)),
         (grid_ref.at[f, :, first_y], hy_ref.at[f, 1], (gx, down_y)),
+        (grid_ref.at[f, sent_low, last_y], hc_ref.at[f, 0, low], (up_x, up_y)),
+        (grid_ref.at[f, sent_low, first_y], hc_ref.at[f, 1, low], (up_x, down_y)),
+        (grid_ref.at[f, sent_high, last_y], hc_ref.at[f, 2, high], (down_x, up_y)),
+        (grid_ref.at[f, sent_high, first_y], hc_ref.at[f, 3, high], (down_x, down_y)),
     ]
+    if f:
+        near = [
+            (grid_ref.at[f, pl.ds(CX - 1, 1)], hx_ref.at[f, 0, pl.ds(XH - 1, 1)], (up_x, gy)),
+            (grid_ref.at[f, pl.ds(0, 1)], hx_ref.at[f, 1, pl.ds(0, 1)], (down_x, gy)),
+        ]
+        far = [
+            (grid_ref.at[f, pl.ds(CX - XH, XH - 1)], hx_ref.at[f, 0, pl.ds(0, XH - 1)], (up_x, gy)),
+            (grid_ref.at[f, pl.ds(1, XH - 1)], hx_ref.at[f, 1, pl.ds(1, XH - 1)], (down_x, gy)),
+        ]
+        plan = near + plan[:2] + far + plan[2:]
+    else:
+        plan = plan + [
+            (grid_ref.at[f, sent_low], hx_ref.at[f, 0, low], (up_x, gy)),
+            (grid_ref.at[f, sent_high], hx_ref.at[f, 1, high], (down_x, gy)),
+        ]
     return [
         remote(src, dst, send_sem.at[f, n], recv_sem.at[f, n], who)
         for n, (src, dst, who) in enumerate(plan)
     ]
 
 
-def spread_halo(f, ext, hx_ref, hy_ref, hc_ref):
-    own_x, own_y = pl.ds(XH, CX), pl.ds(YH, CY)
-    for side, at in ((0, 0), (1, XH + CX)):
-        ext[f, pl.ds(at, XH), own_y] = hx_ref[f, side]
+def spread_y(f, ext, hy_ref):
     for side, at in ((0, 0), (1, YH + CY)):
-        ext[f, own_x, pl.ds(at, YH)] = hy_ref[f, side]
-    for n, (atx, aty) in enumerate(
-        ((0, 0), (0, YH + CY), (XH + CX, 0), (XH + CX, YH + CY))
-    ):
-        ext[f, pl.ds(atx, XH), pl.ds(aty, YH)] = hc_ref[f, n]
+        ext[f, pl.ds(XH, CX), pl.ds(at, YH)] = hy_ref[f, side]
+
+
+def spread_near(ext, hx_ref):
+    own_y = pl.ds(YH, CY)
+    ext[1, XH - 1, own_y] = hx_ref[1, 0, XH - 1]
+    ext[1, XH + CX, own_y] = hx_ref[1, 1, 0]
+
+
+def spread_x(f, ext, hx_ref, hc_ref):
+    deep = XH if f else XH - 1
+    for side, skip, at in ((0, XH - deep, XH - deep), (1, 0, XH + CX)):
+        planes, from_planes = pl.ds(at, deep), pl.ds(skip, deep)
+        ext[f, planes, pl.ds(YH, CY)] = hx_ref[f, side, from_planes]
+        ext[f, planes, pl.ds(0, YH)] = hc_ref[f, 2 * side, from_planes]
+        ext[f, planes, pl.ds(YH + CY, YH)] = hc_ref[f, 2 * side + 1, from_planes]
 
 
 def z_lower(v):
@@ -299,7 +321,7 @@
     return (2.0 / 3.0) / (a + b)
 
 
-def coefficients(ext, w):
+def plane_coefficients(ext, w):
     gx, gy = lax.axis_index("gx"), lax.axis_index("gy")
     shape = (EY, 128)
     row = lax.broadcasted_iota(jnp.int32, shape, 0)
@@ -332,18 +354,18 @@
         own = jnp.broadcast_to((x >= XH) & (x < XH + CX), shape)
         return jnp.minimum(low, jnp.where(own, k * inverse, 1.0))
 
-    def pair(n, low):
-        return plane(2 + 2 * n, plane(1 + 2 * n, low))
-
-    low = lax.fori_loop(0, (EX - 2) // 2, pair, jnp.ones(shape, F32))
+    return plane
+
+
+def lowest_of(low):
     low = jnp.min(low[YH : YH + CY], axis=0, keepdims=True)
-    return jnp.min(low, axis=1, keepdims=True)
+    return jnp.broadcast_to(jnp.min(low, axis=1, keepdims=True), (1, 128))
 
 
 def powers(ext, w, v):
     for x in range(1, EX - 1):
         v[0, x] = w[6, x] * ext[0, x]
-    for n, width in enumerate((4, 2, 4, 3)):
+    for n, width in enumerate((8, 11, 10, 9)):
         count = (EX - 4 - 2 * n) // width
 
         def several(m, _, n=n, width=width):
@@ -384,8 +406,19 @@
     inc[CX + 1] = jnp.where(jnp.broadcast_to(gx == 15, shape), inc[CX], inc[CX + 1])
 
 
+def make_select(keys_ref, table_ref):
+    row = lax.broadcasted_iota(jnp.int32, (128, 256), 0)
+    for h in range(2):
+        key = keys_ref[h : h + 1, :]
+        for v in range(BY):
+            for l in range(6):
+                taken = jnp.where(row == key - (l * 128 - 4 * v), 1.0, 0.0)
+                table_ref[h, v, l * 128 : l * 128 + 128] = taken.astype(BF16)
+
+
 def cut_windows(inc, table_ref, win):
     edge = lax.broadcasted_iota(jnp.int32, (32, 128), 0)
+    both = []
     for h in range(2):
         pieces = [[] for _ in range(6)]
         for u in range(BX):
@@ -397,18 +430,40 @@
                 pieces[l + 1].append(part[l])
             pieces[5].append(jnp.where(edge == 31, part[3], pltpu.roll(part[0], 31, 0)))
         rows = jnp.concatenate([jnp.concatenate(p, axis=0) for p in pieces], axis=1)
-        high, low = halves(rows)
-        for v in range(BY):
-            table = table_ref[v]
-            top, rest = halves(dot(high, table) + dot(low, table))
-            win[0, v * 128 : v * 128 + 128, h * 128 : h * 128 + 128] = top
-            win[1, v * 128 : v * 128 + 128, h * 128 : h * 128 + 128] = rest
+        both.append(jnp.concatenate(halves(rows), axis=0))
+    for v in range(BY):
+        value = dot(both[0], table_ref[0, v]) + dot(both[1], table_ref[1, v])
+        top, rest = halves(value[:128] + value[128:])
+        win[0, v * 128 : v * 128 + 128] = top
+        win[1, v * 128 : v * 128 + 128] = rest
+
+
+def pack_lines(block):
+    top = block[:, :128].reshape(16, PAD, 128)[:, :CAP]
+    rest = block[:, 128:].reshape(16, PAD, 128)
+    last = rest[:, 8:].reshape(128, 128)
+    moved = [pltpu.roll(last, 88 - 30 * p, 1).reshape(16, 8, 128) for p in range(3)]
+    tail = [moved[n % 3][:, 1 + n // 3 : 2 + n // 3] for n in range(9)]
+    lower = jnp.where(lanes((16, 9, 128)) < 88, rest[:, :9], jnp.concatenate(tail, axis=1))
+    return top, lower
+
+
+def unpack_lines(lines):
+    lower = lines[:, CAP:]
+    pieces = [
+        jnp.concatenate([lower[:, 3 * j + p : 3 * j + p + 1] for j in range(3)], axis=1)
+        for p in range(3)
+    ]
+    pieces = [pltpu.roll(x, (30 * p - 88) % 128, 2) for p, x in enumerate(pieces)]
+    lane = lanes((16, 3, 128))
+    last = jnp.where(lane < 30, pieces[0], jnp.where(lane < 60, pieces[1], pieces[2]))
+    return padded_rows(lines[:, :CAP]), padded_rows(jnp.concatenate([lower, last], axis=1))
 
 
 def couple_kernel(
-    t_hbm, k_hbm, depth_hbm, boxes_hbm, places_hbm, average_hbm, select_hbm,
+    t_hbm, k_hbm, depth_hbm, boxes_hbm, places_hbm, average_hbm, keys_hbm,
     mine_ref, glow_ref, k_ref,
-    t_ref, depth_ref, boxes_ref, places_ref, average_ref, first_ref, select_ref,
+    t_ref, depth_ref, boxes_ref, places_ref, average_ref, keys_ref, select_ref,
     back_ref, target_ref, target_c, depths, held, source_ref, outgoing, arrived, grid_ref, hx, hy, hc, ext, w, v,
     low_ref, lows, inc, win, leaving,
     t_sem, k_sem, small_sem,
@@ -421,7 +476,7 @@
     def block_copies(step):
         rows = pl.ds(pl.multiple_of(step * ROWS, ROWS), ROWS)
         return (
-            pltpu.make_async_copy(t_hbm.at[rows], t_ref.at[rows], t_sem.at[step]),
+            pltpu.make_async_copy(t_hbm.at[rows], t_ref.at[step % 3], t_sem.at[step]),
             pltpu.make_async_copy(k_hbm.at[rows], k_ref.at[rows], k_sem.at[step]),
         )
 
@@ -433,7 +488,7 @@
                 (boxes_hbm, boxes_ref),
                 (places_hbm, places_ref),
                 (average_hbm, average_ref),
-                (select_hbm, first_ref),
+                (keys_hbm, keys_ref),
             )
         )
     ]
@@ -481,11 +536,7 @@
         target_c[n * ROWS : n * ROWS + ROWS, :] = column(target[:, n * ROWS : n * ROWS + ROWS])
     source = source_ref[...]
     small[4].wait()
-    for l in range(6):
-        table = first_ref[l].astype(F32)
-        for v_at in range(BY):
-            moved = pltpu.roll(table, 4 * v_at, 0) if v_at else table
-            select_ref[v_at, l * 128 : l * 128 + 128] = moved.astype(BF16)
+    make_select(keys_ref, select_ref)
     assemble(arrived, out_recv, source, base, grid_ref)
     ext[1, pl.ds(XH, CX), pl.ds(YH, CY)] = grid_ref[1]
     copies = [
@@ -493,24 +544,42 @@
     ]
     for copy in copies[1]:
         copy.start()
-    ext[0, pl.ds(XH, CX), pl.ds(YH, CY)] = grid_ref[0]
     for copy in copies[1]:
         copy.wait_send()
     for copy in copies[0]:
         copy.start()
-    for copy in copies[1]:
+    plane = plane_coefficients(ext, w)
+    for copy in copies[1][2:4]:
         copy.wait_recv()
-    spread_halo(1, ext, hx, hy, hc)
-    low_ref[...] = jnp.broadcast_to(coefficients(ext, w), (1, 128))
-    for copy in copies[0][6:]:
-        copy.wait()
+    spread_y(1, ext, hy)
+    low = lax.fori_loop(
+        0,
+        (CX - 2) // 2,
+        lambda n, low: plane(XH + 2 + 2 * n, plane(XH + 1 + 2 * n, low)),
+        jnp.ones((EY, 128), F32),
+    )
+    for copy in copies[1][:2]:
+        copy.wait_recv()
+    spread_near(ext, hx)
+    low_ref[...] = lowest_of(plane(XH + CX - 1, plane(XH, low)))
+    ext[0, pl.ds(XH, CX), pl.ds(YH, CY)] = grid_ref[0]
     ids = peer_ids()
     for q in sorted(range(1, NDEV), key=lambda q: -hops(q)):
         remote(low_ref, lows.at[q], low_send, low_recv, ids[q]).start()
     lows[0] = low_ref[...]
-    for copy in copies[0][:6]:
+    for copy in copies[1][4:]:
+        copy.wait_recv()
+    spread_x(1, ext, hx, hc)
+
+    def outer_pair(n, low):
+        x = 1 + 2 * n + (CX - 2) * (n // 3)
+        return plane(x + 1, plane(x, low))
+
+    lax.fori_loop(0, XH, outer_pair, low)
+    for copy in copies[0]:
         copy.wait()
-    spread_halo(0, ext, hx, hy, hc)
+    spread_y(0, ext, hy)
+    spread_x(0, ext, hx, hc)
     powers(ext, w, v)
     others = pl.ds(1, NDEV - 1)
     pltpu.make_async_copy(lows.at[others], lows.at[others], low_recv).wait()
@@ -522,17 +591,15 @@
         return dot(hot, win[0]) + dot(hot, win[1])
 
     def put_back(c, block):
-        for h in range(2):
-            part = block[:, h * 128 : h * 128 + 128].reshape(16, PAD, 128)
-            leaving[16 * c : 16 * c + 16, h] = part[:, :CAP]
+        top, lower = pack_lines(block)
+        leaving[16 * c : 16 * c + 16, :CAP] = top
+        leaving[16 * c : 16 * c + 16, CAP:] = lower
 
     send_out(leaving, to_slots, put_back, back_ref, back_send, back_recv)
     across = place_index((1, 256), 1, me)
     for c in CHUNKS:
         wait_chunk(back_ref, back_recv, c)
-        parts = [
-            halves(padded_rows(back_ref[16 * c : 16 * c + 16, h])) for h in range(2)
-        ]
+        parts = [halves(part) for part in unpack_lines(back_ref[16 * c : 16 * c + 16])]
         rows = jnp.concatenate([part[k] for k in range(2) for part in parts], axis=1)
         index = jnp.bitwise_xor(across, c * PAD).astype(F32)
         for n in range(steps):
@@ -553,22 +620,32 @@
     pltpu.make_async_copy(leaving.at[others], leaving.at[others], back_send).wait()
 
 
-def prolong_kernel(mine_ref, k_ref, glow_ref, twice_ref, plane_ref, out_ref):
-    step = pl.program_id(0)
-    at_row = pl.ds(pl.multiple_of(step * ROWS, ROWS), ROWS)
-    both = dot(mine_ref[at_row, :], twice_ref[...])
+def prolong_kernel(mine_ref, k_ref, glow_ref, twice_ref, plane_ref, out_hbm, out_ref, sem):
     first = lanes((ROWS, 128)) < 64
     weights = line_weights()
-    plane = plane_ref[...]
-    for a in range(16):
-        low = int(np.flatnonzero(weights[a])[0])
-        value = float(weights[a, low]) * both[:, low * 128 : low * 128 + 128] + float(
-            weights[a, low + 1]
-        ) * both[:, low * 128 + 128 : low * 128 + 256]
-        rest = value - value.astype(BF16).astype(F32)
-        fine = dot(jnp.where(first, value, rest).astype(BF16), plane)
-        at = slice(a * 256, a * 256 + 256)
-        out_ref[:, at] = k_ref[at_row, at].astype(F32) * fine - glow_ref[at_row, at]
+
+    def copy_out(step):
+        rows = pl.ds(pl.multiple_of(step * ROWS, ROWS), ROWS)
+        return pltpu.make_async_copy(out_ref.at[rows], out_hbm.at[rows], sem.at[step])
+
+    @pl.loop(0, SLOTS // ROWS)
+    def _(step):
+        at_row = pl.ds(pl.multiple_of(step * ROWS, ROWS), ROWS)
+        both = dot(mine_ref[at_row, :], twice_ref[...])
+        plane = plane_ref[...]
+        for a in range(16):
+            low = int(np.flatnonzero(weights[a])[0])
+            value = float(weights[a, low]) * both[:, low * 128 : low * 128 + 128] + float(
+                weights[a, low + 1]
+            ) * both[:, low * 128 + 128 : low * 128 + 256]
+            rest = value - value.astype(BF16).astype(F32)
+            fine = dot(jnp.where(first, value, rest).astype(BF16), plane)
+            at = slice(a * 256, a * 256 + 256)
+            out_ref[at_row, at] = k_ref[at_row, at].astype(F32) * fine - glow_ref[at_row, at]
+        copy_out(step).start()
+
+    for step in range(SLOTS // ROWS):
+        copy_out(step).wait()
 
 
 VM = pl.BlockSpec(memory_space=pltpu.VMEM)
@@ -583,7 +660,6 @@
 def on_device(thermal_state, opacity_field, glowing_depth, position_to_tile, tile_to_position):
     dma = pltpu.SemaphoreType.DMA
     steps = SLOTS // ROWS
-    wide = pl.BlockSpec((ROWS, 4096), lambda i: (i, 0))
 
     def vmem(*shape, dtype=F32):
         return pltpu.VMEM(shape, dtype)
@@ -598,14 +674,14 @@
         in_specs=[HB] * 7,
         out_specs=[VM] * 3,
         scratch_shapes=[
-            vmem(SLOTS, 4096, dtype=BF16),
+            vmem(3, ROWS, 4096, dtype=BF16),
             vmem(SLOTS, dtype=jnp.int32),
             vmem(SLOTS, dtype=jnp.int32),
             vmem(SLOTS, dtype=jnp.int32),
             vmem(8, 256, 128, dtype=BF16),
-            vmem(6, 128, 128, dtype=BF16),
-            vmem(BY, 768, 128, dtype=BF16),
-            vmem(NDEV, 2, CAP, 128),
+            vmem(8, 256, dtype=jnp.int32),
+            vmem(2, BY, 768, 256, dtype=BF16),
+            vmem(NDEV, LINES, 128),
             vmem(1, SLOTS),
             vmem(SLOTS, 128),
             vmem(8, 128),
@@ -624,14 +700,14 @@
             vmem(NDEV, 1, 128),
             vmem(CX + 2, EY, 128),
             vmem(2, SLOTS, 256, dtype=BF16),
-            vmem(NDEV, 2, CAP, 128),
+            vmem(NDEV, LINES, 128),
             dma((steps,)),
             dma((steps,)),
             dma((5,)),
             dma,
             dma((8,)),
-            dma((2, 8)),
-            dma((2, 8)),
+            dma((2, 10)),
+            dma((2, 10)),
             dma,
             dma,
             dma,
@@ -651,16 +727,16 @@
                 position_to_tile,
                 tile_to_position,
                 average_table(),
-                select_table(),
+                select_keys(),
             )
         )
     )
     return pl.pallas_call(
         prolong_kernel,
         out_shape=struct(SLOTS, 4096),
-        grid=(steps,),
         in_specs=[VM] * 5,
-        out_specs=wide,
+        out_specs=pl.BlockSpec(memory_space=pltpu.HBM),
+        scratch_shapes=[vmem(SLOTS, 4096), dma((steps,))],
         compiler_params=pltpu.CompilerParams(vmem_limit_bytes=20 * MIB),
         name="prolong",
     )(

time: 71.3 us -> 66.2 us (0.928)
  Pallas kernels: 71.1 us -> 65.8 us
    pallas_call x1, Pallas kernels: 64.1 us -> 59.9 us  [on_device(): pl.pallas_call(couple_kernel, out_shape=[vmem(SLOTS, 512, dtype=BF16), vm...]
    pallas_call x1, Pallas kernels: 7.06 us -> 5.93 us  [on_device(): pl.pallas_call(prolong_kernel, out_shape=struct(SLOTS, 4096), in_specs=[V...]
where the time goes in v4:
time: 66.2 us; the launch traced here: 66 us
  Pallas kernels  65.8 us (99%)
    pallas_call x1, Pallas kernels, on_device(): pl.pallas_call(couple_kernel, out_shape=[vmem(SLOTS, 512, dtype=BF16), vm...  59.9 us
    pallas_call x1, Pallas kernels, on_device(): pl.pallas_call(prolong_kernel, out_shape=struct(SLOTS, 4096), in_specs=[V...  5.93 us

profile of v4, /device:TPU:1, one launch (start us, length us, event | category | flops | bytes accessed | tf_op | source)
XLA Modules:
  0.0 66.0 jit_solution(17499489337370550627)
XLA Ops:
  0.0 0.0 copy-start
  0.0 0.0 copy-start.1
  0.0 59.9 %couple.1 = (bf16[768,512]{1,0:T(8,128)(2,1)S(1)}, f32[768,4096]{1,0:T(8,128)S(1)}, bf16[768,4096]{1,0:T(8,128)(2,1)S(1)}) custom-call(bf16[768,4096]{1,0:T(8,128)(2,1)} %t_hbm.1, bf16[768,4096]{1,0:T(8,128)(2,1)} %k_hbm.1, s32[768]{0:T(1024)} %depth_hbm.1, s32[768]{0:T(1024)} %boxes_hbm.1, s32[768]{0:T(1024)} %places_hbm.1, ...), custom_call_target="tpu_custom_call" | custom-call | tf_op jit(solution)/shard_map/couple/pallas_call | solution.py:667
  59.9 0.0 copy-done
  59.9 0.0 copy-done.1
  59.9 5.9 %prolong.1 = f32[768,4096]{1,0:T(8,128)} custom-call(bf16[768,512]{1,0:T(8,128)(2,1)S(1)} %get-tuple-element.8.mine_ref, bf16[768,4096]{1,0:T(8,128)(2,1)S(1)} %get-tuple-element.9.k_ref, f32[768,4096]{1,0:T(8,128)S(1)} %get-tuple-element.10.glow_ref, bf16[512,768]{1,0:T(8,128)(2,1)S(1)} %copy-done, bf16[128,256]{1,0:T(8,128)(2,1)S(1)} %copy-done.1), custom_call_target="tpu_custom_call" | custom-call | tf_op jit(solution)/shard_map/prolong/pallas_call | solution.py:734
Async XLA Ops:
  0.0 59.9 %copy-start = (bf16[512,768]{1,0:T(8,128)(2,1)S(1)}, bf16[512,768]{1,0:T(8,128)(2,1)}, u32[]{:S(2)}) copy-start(bf16[512,768]{1,0:T(8,128)(2,1)} %constant.10.clone.twice_ref) | copy-start | bytes 2359300
  0.0 59.9 %copy-start.1 = (bf16[128,256]{1,0:T(8,128)(2,1)S(1)}, bf16[128,256]{1,0:T(8,128)(2,1)}, u32[]{:S(2)}) copy-start(bf16[128,256]{1,0:T(8,128)(2,1)} %constant.11.clone.plane_ref) | copy-start | bytes 196612

commit v5 on v4

--- a/solution.py
+++ b/solution.py
@@ -100,23 +100,32 @@
 
 
 CHUNKS = range(8)
+UPPER = [
+    x * 64 + y * 16 + z * 4
+    for x, y, z in (
+        (1, 1, 1), (1, 1, 0), (1, 0, 1), (0, 1, 1), (1, 0, 0), (0, 1, 0), (0, 0, 1), (0, 0, 0)
+    )
+]
+OWN = 112
+
+
+def lower_bits(t):
+    return t // 8 * 32 + t // 4 % 2 * 8 + t % 4
 
 
 def peer_of(block):
-    t = block % 16
-    return t * 8 + (block // 16 ^ t % 8)
+    return UPPER[block // 16] + lower_bits(block % 16)
 
 
 def chunk_blocks(c):
     return sorted(
-        (n for n in range(16 * c, 16 * c + 16) if n), key=lambda n: -hops(peer_of(n))
+        (n for n in range(16 * c, 16 * c + 16) if n != OWN), key=lambda n: -hops(peer_of(n))
     )
 
 
-def place_index(shape, dim, me, start=0):
-    row = lax.broadcasted_iota(jnp.int32, shape, dim) + start
-    t = row // PAD % 16
-    peer = jnp.bitwise_xor(t * 8 + jnp.bitwise_xor(t % 8, row // 256), jnp.broadcast_to(me, shape))
+def place_index(shape, dim, me):
+    row = lax.broadcasted_iota(jnp.int32, shape, dim)
+    peer = jnp.bitwise_xor(lower_bits(row // PAD), jnp.broadcast_to(me, shape))
     return peer * PAD + row % PAD
 
 
@@ -168,7 +177,7 @@
 
 
 def one_hot(row, base, c):
-    index = jnp.bitwise_xor(base, c * PAD).astype(F32)
+    index = jnp.bitwise_xor(base, UPPER[c] * PAD).astype(F32)
     return jnp.concatenate(
         [
             jnp.where(index == row[:, n * 128 : n * 128 + 128], 1.0, 0.0).astype(BF16)
@@ -214,11 +223,11 @@
                     x_ref.at[n], o_ref.at[n], send_sem, recv_sems.at[before], ids[peer_of(n)]
                 ).start()
         before = c
-    o_ref[0] = x_ref[0]
+    o_ref[OWN] = x_ref[OWN]
 
 
 def wait_chunk(o_ref, recv_sems, c):
-    blocks = pl.ds(1, 15) if c == 0 else pl.ds(16 * c, 16)
+    blocks = pl.ds(OWN + 1, 15) if c == OWN // 16 else pl.ds(16 * c, 16)
     pltpu.make_async_copy(o_ref.at[blocks], o_ref.at[blocks], recv_sems.at[c]).wait()
 
 
@@ -601,7 +610,7 @@
         wait_chunk(back_ref, back_recv, c)
         parts = [halves(part) for part in unpack_lines(back_ref[16 * c : 16 * c + 16])]
         rows = jnp.concatenate([part[k] for k in range(2) for part in parts], axis=1)
-        index = jnp.bitwise_xor(across, c * PAD).astype(F32)
+        index = jnp.bitwise_xor(across, UPPER[c] * PAD).astype(F32)
         for n in range(steps):
             at = slice(n * ROWS, n * ROWS + ROWS)
             hot = jnp.concatenate(

time: 66.2 us -> 67.8 us (1.024)
  Pallas kernels: 65.8 us -> 67.4 us
    pallas_call x1, Pallas kernels: 59.9 us -> 61.5 us  [on_device(): pl.pallas_call(couple_kernel, out_shape=[vmem(SLOTS, 512, dtype=BF16), vm...]
where the time goes in v5:
time: 67.8 us; the launch traced here: 67.6 us
  Pallas kernels  67.4 us (99%)
    pallas_call x1, Pallas kernels, on_device(): pl.pallas_call(couple_kernel, out_shape=[vmem(SLOTS, 512, dtype=BF16), vm...  61.5 us
    pallas_call x1, Pallas kernels, on_device(): pl.pallas_call(prolong_kernel, out_shape=struct(SLOTS, 4096), in_specs=[V...  5.95 us

profile of v5, /device:TPU:1, one launch (start us, length us, event | category | flops | bytes accessed | tf_op | source)
XLA Modules:
  0.0 67.6 jit_solution(82447930158348619)
XLA Ops:
  0.0 0.0 copy-start
  0.0 0.0 copy-start.1
  0.0 61.5 %couple.1 = (bf16[768,512]{1,0:T(8,128)(2,1)S(1)}, f32[768,4096]{1,0:T(8,128)S(1)}, bf16[768,4096]{1,0:T(8,128)(2,1)S(1)}) custom-call(bf16[768,4096]{1,0:T(8,128)(2,1)} %t_hbm.1, bf16[768,4096]{1,0:T(8,128)(2,1)} %k_hbm.1, s32[768]{0:T(1024)} %depth_hbm.1, s32[768]{0:T(1024)} %boxes_hbm.1, s32[768]{0:T(1024)} %places_hbm.1, ...), custom_call_target="tpu_custom_call" | custom-call | tf_op jit(solution)/shard_map/couple/pallas_call | solution.py:676
  61.5 0.0 copy-done
  61.5 0.0 copy-done.1
  61.5 5.9 %prolong.1 = f32[768,4096]{1,0:T(8,128)} custom-call(bf16[768,512]{1,0:T(8,128)(2,1)S(1)} %get-tuple-element.8.mine_ref, bf16[768,4096]{1,0:T(8,128)(2,1)S(1)} %get-tuple-element.9.k_ref, f32[768,4096]{1,0:T(8,128)S(1)} %get-tuple-element.10.glow_ref, bf16[512,768]{1,0:T(8,128)(2,1)S(1)} %copy-done, bf16[128,256]{1,0:T(8,128)(2,1)S(1)} %copy-done.1), custom_call_target="tpu_custom_call" | custom-call | tf_op jit(solution)/shard_map/prolong/pallas_call | solution.py:743
Async XLA Ops:
  0.0 61.5 %copy-start = (bf16[512,768]{1,0:T(8,128)(2,1)S(1)}, bf16[512,768]{1,0:T(8,128)(2,1)}, u32[]{:S(2)}) copy-start(bf16[512,768]{1,0:T(8,128)(2,1)} %constant.10.clone.twice_ref) | copy-start | bytes 2359300
  0.0 61.5 %copy-start.1 = (bf16[128,256]{1,0:T(8,128)(2,1)S(1)}, bf16[128,256]{1,0:T(8,128)(2,1)}, u32[]{:S(2)}) copy-start(bf16[128,256]{1,0:T(8,128)(2,1)} %constant.11.clone.plane_ref) | copy-start | bytes 196612

commit v6 on v4

--- a/solution.py
+++ b/solution.py
@@ -1,3 +1,5 @@
+import random
+
 import jax
 import jax.numpy as jnp
 import numpy as np
@@ -108,9 +110,9 @@
 
 
 def chunk_blocks(c):
-    return sorted(
-        (n for n in range(16 * c, 16 * c + 16) if n), key=lambda n: -hops(peer_of(n))
-    )
+    blocks = [n for n in range(16 * c, 16 * c + 16) if n]
+    random.Random(c).shuffle(blocks)
+    return blocks
 
 
 def place_index(shape, dim, me, start=0):

time: 66.2 us -> 66.6 us (level)
  no operation moved by 1% of the time
where the time goes in v6:
time: 66.6 us; the launch traced here: 66.4 us
  Pallas kernels  66.2 us (99%)
    pallas_call x1, Pallas kernels, on_device(): pl.pallas_call(couple_kernel, out_shape=[vmem(SLOTS, 512, dtype=BF16), vm...  60.3 us
    pallas_call x1, Pallas kernels, on_device(): pl.pallas_call(prolong_kernel, out_shape=struct(SLOTS, 4096), in_specs=[V...  5.93 us

profile of v6, /device:TPU:1, one launch (start us, length us, event | category | flops | bytes accessed | tf_op | source)
XLA Modules:
  0.0 66.4 jit_solution(3117128147787806406)
XLA Ops:
  0.0 0.0 copy-start
  0.0 0.0 copy-start.1
  0.0 60.3 %couple.1 = (bf16[768,512]{1,0:T(8,128)(2,1)S(1)}, f32[768,4096]{1,0:T(8,128)S(1)}, bf16[768,4096]{1,0:T(8,128)(2,1)S(1)}) custom-call(bf16[768,4096]{1,0:T(8,128)(2,1)} %t_hbm.1, bf16[768,4096]{1,0:T(8,128)(2,1)} %k_hbm.1, s32[768]{0:T(1024)} %depth_hbm.1, s32[768]{0:T(1024)} %boxes_hbm.1, s32[768]{0:T(1024)} %places_hbm.1, ...), custom_call_target="tpu_custom_call" | custom-call | tf_op jit(solution)/shard_map/couple/pallas_call | solution.py:669
  60.3 0.0 copy-done
  60.3 0.0 copy-done.1
  60.3 5.9 %prolong.1 = f32[768,4096]{1,0:T(8,128)} custom-call(bf16[768,512]{1,0:T(8,128)(2,1)S(1)} %get-tuple-element.8.mine_ref, bf16[768,4096]{1,0:T(8,128)(2,1)S(1)} %get-tuple-element.9.k_ref, f32[768,4096]{1,0:T(8,128)S(1)} %get-tuple-element.10.glow_ref, bf16[512,768]{1,0:T(8,128)(2,1)S(1)} %copy-done, bf16[128,256]{1,0:T(8,128)(2,1)S(1)} %copy-done.1), custom_call_target="tpu_custom_call" | custom-call | tf_op jit(solution)/shard_map/prolong/pallas_call | solution.py:736
Async XLA Ops:
  0.0 60.3 %copy-start = (bf16[512,768]{1,0:T(8,128)(2,1)S(1)}, bf16[512,768]{1,0:T(8,128)(2,1)}, u32[]{:S(2)}) copy-start(bf16[512,768]{1,0:T(8,128)(2,1)} %constant.10.clone.twice_ref) | copy-start | bytes 2359300
  0.0 60.3 %copy-start.1 = (bf16[128,256]{1,0:T(8,128)(2,1)S(1)}, bf16[128,256]{1,0:T(8,128)(2,1)}, u32[]{:S(2)}) copy-start(bf16[128,256]{1,0:T(8,128)(2,1)} %constant.11.clone.plane_ref) | copy-start | bytes 196612
